TPU v7x, 32 devices: a whole 2x2x4 slice. The times are simulated.
32 devices in a mesh: dp: 8 (over y, x, core), seq: 4 (over z).
Axes of the slice: x: 2, y: 2, z: 4, core: 2. Of those that a mesh axis runs over, the one named last changes fastest.
Arguments:
- tokens: bfloat16 [8, 512, 1024], P('dp', 'seq'), may hold values from -6 to 6
- cotangent: bfloat16 [8, 512, 1024], P('dp', 'seq'), may hold values from -6 to 6
- stamps: int32 [8, 512], P('dp'), may hold values from 0 to 1080832, as said below
- lengths: int32 [8], P('dp'), may hold values from 64 to 512, as said below
- w_qkvu: bfloat16 [1024, 4096], P('dp'), may hold values from -0.1875 to 0.1875
- w_out: bfloat16 [1024, 1024], P('dp'), may hold values from -0.1875 to 0.1875
- gain_in: float32 [1024], replicated, may hold values from 0.25 to 1.75
- gain_out: float32 [1024], replicated, may hold values from 0.25 to 1.75
- bias_table: float32 [8, 16], replicated, may hold values from -4 to 4
Outputs:
- mixed: bfloat16 [8, 512, 1024], P('dp', 'seq')
- input_grad: bfloat16 [8, 512, 1024], P('dp', 'seq')
- out_weight_grad: float32 [1024, 1024], P('dp')
Inputs may be any that keep to these rules, and one draw needn't show every extreme that they name: `lengths`: each stream has 64 valid actions or more; some stream is full. `stamps`: timestamps never fall along a stream, and consecutive ones differ by less than 64.
All inputs are finite; a program needn't handle non-finite values.
Results may differ from a plain program's by a relative error of at most 0.019.
Values may be sent and summed in bfloat16 or wider, within the bound.
A program may use at most 128 MiB of HBM per device.

v0:
```python
import jax
import jax.numpy as jnp
from jax import lax
from jax.experimental import pallas as pl
from jax.experimental.pallas import tpu as pltpu
from jax.sharding import PartitionSpec as P

H = 8
DH = 128


EPS = 1e-05


def layer_norm(values, gain):
    average = jnp.mean(values, axis=-1, keepdims=True)
    centred = values - average
    variance = jnp.mean(centred * centred, axis=-1, keepdims=True)
    return centred * lax.rsqrt(variance + EPS) * gain


def silu_slope(values):
    sigmoid_v = jax.nn.sigmoid(values)
    return sigmoid_v * (1.0 + values * (1.0 - sigmoid_v))


def time_bias(bias_table, stamps_q, stamps_k):
    elapsed = stamps_q[:, None] - stamps_k[None, :]
    bucket = jnp.zeros(elapsed.shape, jnp.int32)
    for degree in range(1, bias_table.shape[1]):
        bucket = bucket + (elapsed >= 2**degree - 1).astype(jnp.int32)
    levels = jnp.arange(bias_table.shape[1], dtype=jnp.int32)
    one_hot = (bucket[:, :, None] == levels[None, None, :]).astype(jnp.float32)
    return jnp.einsum(
        "qkb,hb->hqk",
        one_hot,
        bias_table,
        precision=lax.Precision.HIGHEST,
        preferred_element_type=jnp.float32,
    )


def pair_terms(
    q_heads, d_heads, stamps_q, pos_q, k_heads, v_heads, stamps_k, pos_k, length, bias_table, scale
):
    scores = (
        jnp.einsum("qhd,khd->hqk", q_heads, k_heads, preferred_element_type=jnp.float32) * scale
    )
    scores = scores + time_bias(bias_table, stamps_q, stamps_k)
    allowed = (
        (pos_k[None, :] <= pos_q[:, None]) & (pos_k[None, :] < length) & (pos_q[:, None] < length)
    )
    weight = jnp.where(allowed[None], jax.nn.silu(scores), 0.0).astype(jnp.bfloat16)
    if d_heads is None:
        return (weight, None)
    d_weight = jnp.einsum("qhd,khd->hqk", d_heads, v_heads, preferred_element_type=jnp.float32)
    d_scores = jnp.where(allowed[None], d_weight * silu_slope(scores), 0.0).astype(jnp.bfloat16)
    return (weight, d_scores)


def per_device(tokens, cotangent, stamps, lengths, w_qkvu, w_out, gain_in, gain_out, bias_table):
    rows = tokens[0]
    cot_rows = cotangent[0]
    tok_count = rows.shape[0]
    feature_width = rows.shape[1]
    seq_count = lax.axis_size("seq")
    total_rows = tok_count * seq_count
    first_row = lax.axis_index("seq") * tok_count
    length = lengths[0]
    stamp_all = stamps[0]
    pos_own = first_row + jnp.arange(tok_count, dtype=jnp.int32)
    stamp_own = lax.dynamic_slice_in_dim(stamp_all, first_row, tok_count)
    scale = DH ** (-0.5)
    block_rows = min(512, total_rows)
    block_count = total_rows // block_rows
    w_full, w_out_full = (
        lax.all_gather(w_qkvu, "dp", axis=0, tiled=True),
        lax.all_gather(w_out, "dp", axis=0, tiled=True),
    )
    wide_rows = rows.astype(jnp.float32)
    normed = layer_norm(wide_rows, gain_in).astype(jnp.bfloat16)
    projected = jnp.dot(normed, w_full, preferred_element_type=jnp.float32)
    activated = jax.nn.silu(projected)
    gate_u = activated[:, :feature_width]
    values_own = activated[:, feature_width : 2 * feature_width].astype(jnp.bfloat16)
    queries_own = activated[:, 2 * feature_width : 3 * feature_width].astype(jnp.bfloat16)
    keys_own = activated[:, 3 * feature_width :].astype(jnp.bfloat16)
    keys_all, values_all = (
        lax.all_gather(keys_own, "seq", axis=0, tiled=True),
        lax.all_gather(values_own, "seq", axis=0, tiled=True),
    )
    q_heads = queries_own.reshape(tok_count, H, DH)

    def key_block(start):
        k_heads = lax.dynamic_slice_in_dim(keys_all, start, block_rows).reshape(block_rows, H, DH)
        v_heads = lax.dynamic_slice_in_dim(values_all, start, block_rows).reshape(block_rows, H, DH)
        stamps_k = lax.dynamic_slice_in_dim(stamp_all, start, block_rows)
        pos_k = start + jnp.arange(block_rows, dtype=jnp.int32)
        return (k_heads, v_heads, stamps_k, pos_k)

    def guarded(active, action, state):
        return lax.cond(active, action, lambda same: same, state)

    def reaches(start):
        return (start <= first_row + tok_count - 1) & (start < length) & (first_row < length)

    def forward_step(block_idx, totals):
        start = block_idx * block_rows

        def forward_compute(totals):
            k_heads, v_heads, stamps_k, pos_k = key_block(start)
            weight, unused = pair_terms(
                q_heads,
                None,
                stamp_own,
                pos_own,
                k_heads,
                v_heads,
                stamps_k,
                pos_k,
                length,
                bias_table,
                scale,
            )
            return totals + jnp.einsum(
                "hqk,khd->qhd", weight, v_heads, preferred_element_type=jnp.float32
            )

        return guarded(reaches(start), forward_compute, totals)

    attended = lax.fori_loop(
        0, block_count, forward_step, jnp.zeros((tok_count, H, DH), jnp.float32)
    )
    attended = attended.reshape(tok_count, feature_width)
    normed_att, norm_back = jax.vjp(lambda values: layer_norm(values, gain_out), attended)
    mixed_rows = (normed_att * gate_u).astype(jnp.bfloat16)
    mixed = (
        wide_rows + jnp.dot(mixed_rows, w_out_full, preferred_element_type=jnp.float32)
    ).astype(jnp.bfloat16)
    grad_part = lax.psum_scatter(
        jnp.einsum("tr,tc->rc", mixed_rows, cot_rows, preferred_element_type=jnp.float32).astype(
            jnp.bfloat16
        ),
        "dp",
        scatter_dimension=0,
        tiled=True,
    )
    w_grad = lax.psum(grad_part, "seq").astype(jnp.float32)
    d_mix = jnp.einsum("tc,rc->tr", cot_rows, w_out_full, preferred_element_type=jnp.float32)
    d_gate = d_mix * normed_att
    d_att = norm_back(d_mix * gate_u)[0].astype(jnp.bfloat16)
    d_heads = d_att.reshape(tok_count, H, DH)

    def backward_step():

        def step(block_idx, state_pair):
            start = block_idx * block_rows

            def step_compute(state_pair):
                q_grad, key_terms = state_pair
                k_heads, v_heads, stamps_k, pos_k = key_block(start)
                weight, d_scores = pair_terms(
                    q_heads,
                    d_heads,
                    stamp_own,
                    pos_own,
                    k_heads,
                    v_heads,
                    stamps_k,
                    pos_k,
                    length,
                    bias_table,
                    scale,
                )
                q_grad = (
                    q_grad
                    + jnp.einsum(
                        "hqk,khd->qhd", d_scores, k_heads, preferred_element_type=jnp.float32
                    )
                    * scale
                )
                k_grad = (
                    jnp.einsum(
                        "hqk,qhd->khd", d_scores, q_heads, preferred_element_type=jnp.float32
                    )
                    * scale
                )
                v_grad = jnp.einsum(
                    "hqk,qhd->khd", weight, d_heads, preferred_element_type=jnp.float32
                )
                joined = jnp.concatenate(
                    [
                        k_grad.reshape(block_rows, feature_width),
                        v_grad.reshape(block_rows, feature_width),
                    ],
                    axis=1,
                )
                key_terms = lax.dynamic_update_slice_in_dim(key_terms, joined, start, 0)
                return (q_grad, key_terms)

            return guarded(reaches(start), step_compute, state_pair)

        return step

    q_start = jnp.zeros((tok_count, H, DH), jnp.float32)
    term_start = jnp.zeros((total_rows, 2 * feature_width), jnp.float32)
    q_grad, key_terms = lax.fori_loop(0, block_count, backward_step(), (q_start, term_start))
    key_grads = lax.psum_scatter(
        key_terms.astype(jnp.bfloat16), "seq", scatter_dimension=0, tiled=True
    ).astype(jnp.float32)
    d_act = jnp.concatenate(
        [
            d_gate,
            key_grads[:, feature_width:],
            q_grad.reshape(tok_count, feature_width),
            key_grads[:, :feature_width],
        ],
        axis=1,
    )
    d_proj = (d_act * silu_slope(projected)).astype(jnp.bfloat16)
    d_normed = jnp.einsum("tf,df->td", d_proj, w_full, preferred_element_type=jnp.float32)
    unused_rows, in_back = jax.vjp(lambda values: layer_norm(values, gain_in), wide_rows)
    input_grad = (cot_rows.astype(jnp.float32) + in_back(d_normed)[0]).astype(jnp.bfloat16)
    return (mixed[None], input_grad[None], w_grad)


MESH = pl.DeviceIdType.MESH
VM = pl.BlockSpec(memory_space=pltpu.VMEM)
F32 = jnp.float32
BF16 = jnp.bfloat16


def plane_of(stream):
    chip, core = stream // 2, stream % 2
    mid = 1 - ((chip + 1) // 2) % 2
    return mid * (1 + core) + (1 - mid) * 3 * core


def plane_sources(plane):
    mid = ((plane + 1) // 2) % 2
    core = mid * (plane - 1) + (1 - mid) * (plane // 3)
    return core, (1 - mid, 2 + mid)


def remote(src, dst, send_sem, recv_sem, target):
    return pltpu.make_async_remote_copy(
        src_ref=src,
        dst_ref=dst,
        send_sem=send_sem,
        recv_sem=recv_sem,
        device_id=target,
        device_id_type=MESH,
    )


def gather_kernel(
    n_dp, n_seq, x_ref, c_ref, w_ref, m_ref, gain_ref, proj_ref, co_ref, wo_ref, mo_ref, xo_ref,
    zsend, fsend, frecv, wsend, wrecv, msend, mrecv, local_sem,
):
    me = lax.axis_index("dp")
    z = lax.axis_index("seq")
    chip, core = me // 2, me % 2
    cy, cx = chip // 2, chip % 2
    x_chip, y_chip = 2 * cy + (1 - cx), 2 * (1 - cy) + cx
    sibling = 2 * chip + (1 - core)
    home = plane_of(me)
    slot = chip // 2
    src_core, chips = plane_sources(z)
    ins, outs = (x_ref, c_ref), (xo_ref, co_ref)

    def z_send(a, s):
        return remote(ins[a], outs[a].at[slot, s], zsend.at[a], frecv.at[a, slot, s], (me, home))

    def own_copy(a):
        return pltpu.make_async_copy(ins[a], outs[a].at[slot, z], local_sem.at[a])

    def w_send(peer):
        return remote(w_ref.at[peer], wo_ref.at[me], wsend.at[peer], wrecv.at[me], (peer, z))

    def w_arrive(peer):
        return remote(w_ref.at[peer], wo_ref.at[peer], wsend.at[peer], wrecv.at[peer], (peer, z))

    def w_own():
        return pltpu.make_async_copy(w_ref.at[me], wo_ref.at[me], local_sem.at[3])

    def m_send(peer):
        return remote(m_ref, mo_ref.at[slot], msend.at[peer], mrecv.at[slot], (peer, z))

    def m_own():
        return pltpu.make_async_copy(m_ref, mo_ref.at[slot], local_sem.at[2])

    @pl.when(home != z)
    def _():
        z_send(0, z).start()

    @pl.when(home == z)
    def _():
        own_copy(0).start()
        m_own().start()

    for step in range(1, n_dp):
        peer = lax.rem(me + step, n_dp)

        @pl.when(home == z)
        def _():
            m_send(peer).start()

        w_send(peer).start()
    w_own().start()

    @pl.when(home != z)
    def _():
        z_send(1, z).start()

    @pl.when(home == z)
    def _():
        own_copy(1).start()

    def order(i):
        return lax.rem(z + i, n_seq)

    def pass_on(a, j, b, target, leg):
        block = outs[a].at[j, b]
        return remote(block, block, fsend.at[a, j, b, leg], frecv.at[a, j, b], (target, z))

    def from_source(a, i):
        b = order(i)
        return (
            pass_on(a, slot, b, 2 * x_chip + core, 0),
            pass_on(a, slot, b, 2 * y_chip + core, 1),
            pass_on(a, slot, b, sibling, 2),
        )

    is_source = home == z
    relays = core == src_core

    def relayed(a, i, j):
        b = order(i)
        if i % 2 == 0:
            return relays & (x_chip == chips[j]), pass_on(a, j, b, 2 * y_chip + core, 1)
        return relays & (y_chip == chips[j]), pass_on(a, j, b, 2 * x_chip + core, 0)

    def shared(a, i, j):
        return relays & (chip != chips[j]), pass_on(a, j, order(i), sibling, 2)

    for a in range(2):

        @pl.when(is_source)
        def _():
            for i in range(n_seq):
                if i == 0:
                    own_copy(a).wait()
                else:
                    pass_on(a, slot, order(i), me, 0).wait_recv()
                for copy in from_source(a, i):
                    copy.start()

    def project(i, j):
        b = order(i)
        normed = layer_norm(xo_ref[j, b].astype(F32), gain_ref[...]).astype(BF16)
        weights = wo_ref[...].reshape(-1, 4 * DH)
        proj_ref[j, b] = jnp.dot(normed, weights, preferred_element_type=F32)

    for a in range(2):
        for i in range(n_seq):
            for j in range(2):

                @pl.when(jnp.logical_not(is_source & (slot == j)))
                def _():
                    pass_on(a, j, order(i), me, 0).wait_recv()

                for use, copy in (relayed(a, i, j), shared(a, i, j)):

                    @pl.when(use)
                    def _():
                        copy.start()

                if a == 1:
                    project(i, j)

        if a == 0:
            w_own().wait()
            for step in range(1, n_dp):
                w_arrive(lax.rem(me + step, n_dp)).wait_recv()

    for step in range(1, n_dp):
        peer = lax.rem(me + step, n_dp)
        w_send(peer).wait_send()

        @pl.when(home == z)
        def _():
            m_send(peer).wait_send()

    @pl.when(home == z)
    def _():
        m_own().wait()

    for j in range(2):

        @pl.when(jnp.logical_not((home == z) & (slot == j)))
        def _():
            remote(m_ref, mo_ref.at[j], msend.at[0], mrecv.at[j], (me, z)).wait_recv()

    for a in range(2):

        @pl.when(home != z)
        def _():
            z_send(a, z).wait_send()

        @pl.when(is_source)
        def _():
            for i in range(n_seq):
                for copy in from_source(a, i):
                    copy.wait_send()

        for i in range(n_seq):
            for j in range(2):
                for use, copy in (relayed(a, i, j), shared(a, i, j)):

                    @pl.when(use)
                    def _():
                        copy.wait_send()


def stats_kernel(n_dp, s_ref, o_ref, send, recv, local_sem):
    me = lax.axis_index("dp")
    z = lax.axis_index("seq")
    barrier = pltpu.get_barrier_semaphore()
    for step in range(1, n_dp):
        pl.semaphore_signal(
            barrier, inc=1, device_id=(lax.rem(me + step, n_dp), z), device_id_type=MESH
        )
    pl.semaphore_wait(barrier, n_dp - 1)
    own = pltpu.make_async_copy(s_ref, o_ref.at[me], local_sem)
    own.start()
    for step in range(1, n_dp):
        peer = lax.rem(me + step, n_dp)
        remote(s_ref, o_ref.at[me], send.at[peer], recv.at[me], (peer, z)).start()
    own.wait()
    for step in range(1, n_dp):
        peer = lax.rem(me + step, n_dp)
        copy = remote(s_ref, o_ref.at[peer], send.at[peer], recv.at[peer], (peer, z))
        copy.wait_recv()
        copy.wait_send()


def reduce_kernel(
    n_dp, n_seq, pm_ref, pd_ref, g_ref, o_ref, go_ref, pair, mixed_up, landed, final, g_land, g_sum,
    psend, precv, csend, crecv, osend, orecv, gsend, grecv, hsend, hrecv, local_sem,
):
    me = lax.axis_index("dp")
    z = lax.axis_index("seq")
    chip, core = me // 2, me % 2
    sibling = 2 * chip + (1 - core)
    chips_n = n_dp // 2
    g_rows = g_ref.shape[0] // n_seq
    p_refs = (pm_ref, pd_ref)

    def g_slice(ref, index):
        return ref.at[pl.ds(pl.multiple_of(index * g_rows, g_rows), g_rows)]

    def pair_send(part, c):
        return remote(
            p_refs[part].at[2 * c + (1 - core)], pair.at[part, c],
            psend.at[part, c], precv.at[part, c], (sibling, z),
        )

    def cross_send(part, c):
        return remote(
            mixed_up.at[part, c], landed.at[part, chip],
            csend.at[part, c], crecv.at[part, chip], (2 * c + core, z),
        )

    def cross_arrive(part, c):
        return remote(
            mixed_up.at[part, c], landed.at[part, c],
            csend.at[part, c], crecv.at[part, c], (2 * c + core, z),
        )

    def g_send(peer):
        return remote(
            g_slice(g_ref, peer), g_land.at[z], gsend.at[peer], grecv.at[z], (me, peer)
        )

    def g_arrive(peer):
        return remote(
            g_slice(g_ref, peer), g_land.at[peer], gsend.at[peer], grecv.at[peer], (me, peer)
        )

    def h_send(peer):
        return remote(g_sum, g_slice(go_ref, z), hsend.at[peer], hrecv.at[z], (me, peer))

    def h_arrive(peer):
        return remote(g_sum, g_slice(go_ref, peer), hsend.at[peer], hrecv.at[peer], (me, peer))

    others = [lax.rem(chip + step, chips_n) for step in range(1, chips_n)]
    peers = [lax.rem(z + step, n_seq) for step in range(1, n_seq)]
    parts = len(p_refs)
    for part in range(parts):
        for c in others + [chip]:
            pair_send(part, c).start()
    for peer in peers:
        g_send(peer).start()
    for part in range(parts):
        for c in others + [chip]:
            pair_send(part, c).wait_recv()
            mixed_up[part, c] = (
                p_refs[part][2 * c + core].astype(F32) + pair[part, c].astype(F32)
            ).astype(BF16)
            if c is not chip:
                cross_send(part, c).start()
    total = g_slice(g_ref, z)[...].astype(F32)
    for peer in peers:
        g_arrive(peer).wait_recv()
        total = total + g_land[peer].astype(F32)
    g_sum[...] = total.astype(BF16)
    own_g = pltpu.make_async_copy(g_sum, g_slice(go_ref, z), local_sem.at[0])
    own_g.start()
    for peer in peers:
        h_send(peer).start()
    block, half = me % n_seq, me // n_seq
    src_core, sources = plane_sources(z)
    stream = 2 * ((1 - half) * sources[0] + half * sources[1]) + src_core
    stays = (stream == me) & (block == z)
    gone = jnp.logical_not(stays)
    home = plane_of(me)
    from_dp = (chip // 2) * n_seq + z
    arrives = jnp.logical_not((home == z) & (from_dp == me))

    def final_send(part):
        return remote(
            final.at[part], o_ref.at[part], osend.at[part], orecv.at[part], (stream, block)
        )

    def final_own(part):
        return pltpu.make_async_copy(final.at[part], o_ref.at[part], local_sem.at[1 + part])

    for part in range(parts):
        total = mixed_up[part, chip].astype(F32)
        for c in others:
            cross_arrive(part, c).wait_recv()
            total = total + landed[part, c].astype(F32)
        final[part] = total.astype(BF16)

        @pl.when(gone)
        def _():
            final_send(part).start()

        @pl.when(stays)
        def _():
            final_own(part).start()

    for part in range(parts):
        for c in others + [chip]:
            pair_send(part, c).wait_send()
        for c in others:
            cross_send(part, c).wait_send()

        @pl.when(gone)
        def _():
            final_send(part).wait_send()

        @pl.when(stays)
        def _():
            final_own(part).wait()

        @pl.when(arrives)
        def _():
            final_send(part).wait_recv()

    own_g.wait()
    for peer in peers:
        g_send(peer).wait_send()
        h_send(peer).wait_send()
        h_arrive(peer).wait_recv()


def mm(a, b, dims):
    return lax.dot_general(a, b, (dims, ((), ())), preferred_element_type=F32)


def forward_kernel(
    bias_ref, len_ref, proj_ref, srow_ref, scol_ref, att_ref, weight_ref, slope_ref
):
    length = len_ref[pl.program_id(0)]
    head = lax.axis_index("dp")
    total = proj_ref.shape[1]
    rows = total // 4
    acts = [jax.nn.silu(proj_ref[0, :, (1 + g) * DH : (2 + g) * DH]).astype(BF16) for g in range(3)]
    values, queries, keys = acts
    for start in range(0, total, rows):
        end = start + rows
        scores = mm(queries[start:end], keys[:end], ((1,), (1,))) * DH ** (-0.5)
        elapsed = scol_ref[0, start:end, :] - srow_ref[0, :, :end]
        bias = jnp.full(elapsed.shape, bias_ref[head, 0], F32)
        for degree in range(1, bias_ref.shape[1]):
            bias = jnp.where(elapsed >= 2**degree - 1, bias_ref[head, degree], bias)
        scores = scores + bias
        pos_q = start + lax.broadcasted_iota(jnp.int32, elapsed.shape, 0)
        pos_k = lax.broadcasted_iota(jnp.int32, elapsed.shape, 1)
        allowed = (pos_k <= pos_q) & (pos_k < length) & (pos_q < length)
        sig = jax.nn.sigmoid(scores)
        weight = jnp.where(allowed, scores * sig, 0.0).astype(BF16)
        weight_ref[0, start:end, :end] = weight
        slope_ref[0, start:end, :end] = jnp.where(allowed, sig * (1.0 + scores * (1.0 - sig)), 0.0)
        att_ref[0, start:end, :] = mm(weight, values[:end], ((1,), (0,)))


def backward_kernel(proj_ref, datt_ref, dgate_ref, weight_ref, slope_ref, out_ref, k_acc, v_acc):
    total = proj_ref.shape[1]
    rows = total // 4
    acts = [jax.nn.silu(proj_ref[0, :, (1 + g) * DH : (2 + g) * DH]).astype(BF16) for g in range(3)]
    values, queries, keys = acts
    scale = DH ** (-0.5)

    def put(group, start, end, grad):
        cols = slice(group * DH, (group + 1) * DH)
        out_ref[0, start:end, cols] = (grad * silu_slope(proj_ref[0, start:end, cols])).astype(BF16)

    for start in reversed(range(0, total, rows)):
        end = start + rows
        d_att = datt_ref[0, start:end, :]
        d_weight = mm(d_att, values[:end], ((1,), (1,)))
        d_scores = (d_weight * slope_ref[0, start:end, :end]).astype(BF16)
        put(2, start, end, mm(d_scores, keys[:end], ((1,), (0,))) * scale)
        k_part = mm(d_scores, queries[start:end], ((0,), (0,)))
        v_part = mm(weight_ref[0, start:end, :end], d_att, ((0,), (0,)))
        if end == total:
            k_acc[...] = k_part
            v_acc[...] = v_part
        else:
            k_acc[:end] += k_part
            v_acc[:end] += v_part
    put(0, 0, total, dgate_ref[0])
    put(1, 0, total, v_acc[...])
    put(3, 0, total, k_acc[...] * scale)


def head_parallel(
    n_dp, n_seq, tokens, cotangent, stamps, lengths, w_qkvu, w_out, gain_in, gain_out, bias_table
):
    tok, width = tokens.shape[1:]
    seq_len = stamps.shape[1]
    head = lax.axis_index("dp")
    meta = jnp.concatenate([stamps.reshape(-1, DH), jnp.broadcast_to(lengths[:, None], (4, DH))])
    w_cols = w_qkvu.reshape(-1, 4, n_dp, DH).transpose(2, 0, 1, 3).reshape(n_dp, -1, 4 * DH)
    dma = pltpu.SemaphoreType.DMA
    sds = jax.ShapeDtypeStruct
    side = pltpu.CompilerParams(has_side_effects=True)
    projected, c_all, w_head, metas = pl.pallas_call(
        lambda *refs: gather_kernel(n_dp, n_seq, *refs),
        out_shape=(
            sds((2, n_seq, tok, 4 * DH), F32),
            sds((2, n_seq, tok, width), BF16),
            sds((n_dp, w_qkvu.shape[0], 4 * DH), BF16),
            sds((2,) + meta.shape, jnp.int32),
        ),
        in_specs=[VM] * 5,
        out_specs=[VM] * 4,
        scratch_shapes=[
            pltpu.VMEM((2, n_seq, tok, width), BF16),
            dma((2,)),
            dma((2, 2, n_seq, 3)),
            dma((2, 2, n_seq)),
            dma((n_dp,)),
            dma((n_dp,)),
            dma((n_dp,)),
            dma((2,)),
            dma((4,)),
        ],
        compiler_params=side,
        name="gather",
    )(tokens[0], cotangent[0], w_cols, meta, gain_in[None])
    w_head = w_head.reshape(width, 4 * DH)
    count = 2 * seq_len
    c_rows = c_all.reshape(count, width)
    stamp_rows = metas[:, : seq_len // DH].reshape(2, 1, seq_len)
    stamp_cols = stamp_rows.reshape(2, seq_len, 1)
    spans = metas[:, seq_len // DH, 0]
    projected = projected.reshape(count, 4 * DH)
    proj3 = projected.reshape(2, seq_len, 4 * DH)
    smem = pl.BlockSpec(memory_space=pltpu.SMEM)

    def per(*shape):
        return pl.BlockSpec((1,) + shape, lambda i: (i,) + (0,) * len(shape))

    attended, weight, slope = pl.pallas_call(
        forward_kernel,
        grid=(2,),
        out_shape=(
            sds((2, seq_len, DH), F32),
            sds((2, seq_len, seq_len), BF16),
            sds((2, seq_len, seq_len), F32),
        ),
        in_specs=[smem, smem, per(seq_len, 4 * DH), per(1, seq_len), per(seq_len, 1)],
        out_specs=[per(seq_len, DH), per(seq_len, seq_len), per(seq_len, seq_len)],
        name="forward",
    )(bias_table, spans, proj3, stamp_rows, stamp_cols)
    att = attended.reshape(count, DH)
    gate = jax.nn.silu(projected[:, :DH])
    gain_head = lax.dynamic_slice_in_dim(gain_out, head * DH, DH)
    d_mix = lax.dot_general(c_rows, w_out, (((1,), (1,)), ((), ())), preferred_element_type=F32)
    g = d_mix * gate * gain_head
    mean_own = jnp.mean(att, axis=1)
    off = att - mean_own[:, None]
    stats = jnp.stack(
        [mean_own, jnp.sum(off * off, axis=1), jnp.sum(g, axis=1), jnp.sum(g * off, axis=1)]
    )
    gathered = pl.pallas_call(
        lambda *refs: stats_kernel(n_dp, *refs),
        out_shape=sds((n_dp, 4, count // DH, DH), F32),
        in_specs=[VM],
        out_specs=VM,
        scratch_shapes=[dma((n_dp,)), dma((n_dp,)), dma],
        compiler_params=pltpu.CompilerParams(has_side_effects=True, collective_id=1),
        name="stats",
    )(stats.reshape(4, count // DH, DH))
    means, squares, g_sums, g_offs = [gathered[:, k] for k in range(4)]
    mean = jnp.mean(means, axis=0)
    shift = means - mean[None]
    variance = jnp.sum(squares + DH * shift * shift, axis=0) / width
    rstd = lax.rsqrt(variance + EPS)
    g_mean = jnp.sum(g_sums, axis=0) / width
    g_dot = rstd * jnp.sum(g_offs + shift * g_sums, axis=0) / width
    mean, rstd, g_mean, g_dot = [v.reshape(count, 1) for v in (mean, rstd, g_mean, g_dot)]
    hat = (att - mean) * rstd
    normed_att = hat * gain_head
    mixed_rows = (normed_att * gate).astype(BF16)
    d_gate = d_mix * normed_att
    d_att = (rstd * (g - g_mean - hat * g_dot)).astype(BF16)
    d_proj = pl.pallas_call(
        backward_kernel,
        grid=(2,),
        out_shape=sds((2, seq_len, 4 * DH), BF16),
        in_specs=[
            per(seq_len, 4 * DH),
            per(seq_len, DH),
            per(seq_len, DH),
            per(seq_len, seq_len),
            per(seq_len, seq_len),
        ],
        out_specs=per(seq_len, 4 * DH),
        scratch_shapes=[pltpu.VMEM((seq_len, DH), F32)] * 2,
        name="backward",
    )(proj3, d_att.reshape(2, seq_len, DH), d_gate.reshape(2, seq_len, DH), weight, slope)
    mixed_part = jnp.dot(mixed_rows, w_out, preferred_element_type=F32).astype(BF16)
    d_part = lax.dot_general(
        d_proj.reshape(count, 4 * DH), w_head, (((1,), (1,)), ((), ())), preferred_element_type=F32
    ).astype(BF16)
    w_part = lax.dot_general(
        mixed_rows, c_rows, (((0,), (0,)), ((), ())), preferred_element_type=F32
    ).astype(BF16)
    shape = (n_dp, tok, width)
    half = n_dp // 2
    sums, w_sum = pl.pallas_call(
        lambda *refs: reduce_kernel(n_dp, n_seq, *refs),
        out_shape=(sds((2, tok, width), BF16), sds(w_part.shape, BF16)),
        in_specs=[VM] * 3,
        out_specs=[VM] * 2,
        scratch_shapes=[
            pltpu.VMEM((2, half, tok, width), BF16),
            pltpu.VMEM((2, half, tok, width), BF16),
            pltpu.VMEM((2, half, tok, width), BF16),
            pltpu.VMEM((2, tok, width), BF16),
            pltpu.VMEM((n_seq, w_part.shape[0] // n_seq, width), BF16),
            pltpu.VMEM((w_part.shape[0] // n_seq, width), BF16),
            dma((2, half)),
            dma((2, half)),
            dma((2, half)),
            dma((2, half)),
            dma((2,)),
            dma((2,)),
            dma((n_seq,)),
            dma((n_seq,)),
            dma((n_seq,)),
            dma((n_seq,)),
            dma((3,)),
        ],
        compiler_params=side,
        name="reduce",
    )(mixed_part.reshape(shape), d_part.reshape(shape), w_part)
    wide_rows = tokens[0].astype(F32)
    mixed = (wide_rows + sums[0].astype(F32)).astype(BF16)
    unused_rows, in_back = jax.vjp(lambda values: layer_norm(values, gain_in), wide_rows)
    back = in_back(sums[1].astype(F32))[0]
    input_grad = (cotangent[0].astype(F32) + back).astype(BF16)
    return (mixed[None], input_grad[None], w_sum.astype(F32))


def solution(mesh):
    n_dp, n_seq = mesh.shape["dp"], mesh.shape["seq"]

    def body(*args):
        streams_fit = n_dp == 2 * n_seq and n_dp == H and args[5].shape[0] == DH
        if streams_fit and args[2].shape[0] == 1:
            return head_parallel(n_dp, n_seq, *args)
        return per_device(*args)

    return jax.shard_map(
        body,
        mesh=mesh,
        in_specs=(
            P("dp", "seq", None),
            P("dp", "seq", None),
            P("dp", None),
            P("dp"),
            P("dp", None),
            P("dp", None),
            P(),
            P(),
            P(),
        ),
        out_specs=(P("dp", "seq", None), P("dp", "seq", None), P("dp", None)),
        check_vma=False,
    )
```

profile of v0, /device:TPU:3, one launch (start us, length us, event | category | flops | bytes accessed | tf_op | source)
XLA Modules:
  0.0 159.4 jit_solution(13988979423373660119)
XLA Ops:
  0.6 0.0 copy-start
  0.6 1.5 copy.24
  2.1 0.0 copy-start.9
  2.2 0.4 copy.27
  2.6 1.2 reshape.183.refs_2_
  4.5 0.6 concatenate.4.refs_3_
  5.1 58.0 %gather.1 = (f32[2,4,128,512]{3,2,1,0:T(8,128)}, bf16[2,4,128,1024]{3,2,1,0:T(8,128)(2,1)}, bf16[8,128,512]{2,1,0:T(8,128)(2,1)}, s32[2,8,128]{2,1,0:T(8,128)}) custom-call(bf16[128,1024]{1,0:T(8,128)(2,1)} %bitcast.109, bf16[128,1024]{1,0:T(8,128)(2,1)} %bitcast.119, bf16[8,128,512]{2,1,0:T(8,128)(2,1)} %reshape.183.refs_2_, s32[8,128]{1,0:T(8,128)} %concatenate.4.refs_3_, ...), custom_call_target="tpu_custom_call" | custom-call | tf_op jit(solution)/shard_map/gather/pallas_call | solution.py:650
  63.1 0.8 slice.28
  64.0 1.1 reshape_reshape.8.scol_ref
  65.1 1.3 slice_reduce_fusion.len_ref
  66.4 0.0 copy-done.8
  66.4 5.1 %forward.1 = (f32[2,512,128]{2,1,0:T(8,128)}, bf16[2,512,512]{2,1,0:T(8,128)(2,1)}, f32[2,512,512]{2,1,0:T(8,128)}) custom-call(f32[8,16]{1,0:T(8,128)} %bias_ref.1, s32[2]{0:T(128)} %slice_reduce_fusion.len_ref, f32[2,512,512]{2,1,0:T(8,128)} %bitcast.104, s32[2,1,512]{2,1,0:T(1,128)} %bitcast.121, s32[2,512,1]{2,1,0:T(8,128)} %reshape_reshape.8.scol_ref), custom_call_target="tpu_custom_call" | custom-call | tf_op jit(solution)/shard_map/forward/pallas_call | solution.py:687
  71.5 1.3 reduce_sum.118
  72.8 0.8 dynamic_slice.3
  73.6 0.0 copy-done
  73.6 3.4 %fusion.25 = (f32[1024]{0:T(1024)S(1)}, f32[1024]{0:T(1024)S(1)}, f32[1024,128]{1,0:T(8,128)}, f32[1024,128]{1,0:T(8,128)}) fusion(f32[1024]{0:T(1024)S(1)} %bitcast.122, f32[2,512,128]{2,1,0:T(8,128)} %get-tuple-element.14, f32[128]{0:T(128)S(1)} %dynamic_slice.3, f32[1024,512]{1,0:T(8,128)S(1)} %bitcast.106, bf16[1024,1024]{1,0:T(8,128)(2,1)} %bitcast.112, ...), kind=kOutput, calls=%fused_computation.61 | convolution fusion | flops 269744128 | bytes 4469248 | tf_op jit(solution)/shard_map/dot_general | solution.py:702
  77.0 0.4 multiply_reduce_fusion
  77.4 0.6 pad_maximum_fusion.refs_0_
  78.0 6.4 %stats.1 = f32[8,4,8,128]{3,2,1,0:T(8,128)} custom-call(f32[4,8,128]{2,1,0:T(8,128)} %pad_maximum_fusion.refs_0_), custom_call_target="tpu_custom_call" | custom-call | tf_op jit(solution)/shard_map/stats/pallas_call | solution.py:709
  84.4 0.9 bitcast_reduce_fusion
  85.3 0.8 fusion.20
  86.2 2.6 %multiply_multiply_fusion.1 = (f32[1024,128]{1,0:T(8,128)}, bf16[1024,128]{1,0:T(8,128)(2,1)S(1)}, bf16[1024,128]{1,0:T(8,128)(2,1)}) fusion(f32[1024,128]{1,0:T(8,128)} %get-tuple-element.41, f32[2,512,128]{2,1,0:T(8,128)S(1)} %copy-done.3, f32[1024]{0:T(1024)S(1)} %get-tuple-element.43, f32[1024]{0:T(1024)S(1)} %get-tuple-element.35, ...), kind=kLoop, calls=%fused_computation.36 | loop fusion | flops 1966080 | bytes 3162624 | tf_op jit(solution)/shard_map/mul | solution.py:729
  88.8 1.2 convolution_convert_fusion.2.refs_2_
  90.0 5.2 %backward.1 = bf16[2,512,512]{2,1,0:T(8,128)(2,1)} custom-call(f32[2,512,512]{2,1,0:T(8,128)} %bitcast.105, bf16[2,512,128]{2,1,0:T(8,128)(2,1)} %bitcast.116, f32[2,512,128]{2,1,0:T(8,128)} %bitcast.115, bf16[2,512,512]{2,1,0:T(8,128)(2,1)} %get-tuple-element.16.weight_ref, f32[2,512,512]{2,1,0:T(8,128)} %get-tuple-element.17.slope_ref), custom_call_target="tpu_custom_call" | custom-call | tf_op jit(solution)/shard_map/backward/pallas_call | solution.py:731
  95.2 3.9 %convolution_convert_fusion = bf16[1024,1024]{1,0:T(8,128)(2,1)} fusion(bf16[1024,512]{1,0:T(8,128)(2,1)} %bitcast.117, bf16[1024,512]{1,0:T(8,128)(2,1)S(1)} %bitcast.126), kind=kOutput, calls=%fused_computation | convolution fusion | flops 1074790400 | bytes 4194304 | tf_op jit(solution)/shard_map/dot_general | solution.py:747
  99.0 2.0 %convolution_convert_fusion.1 = bf16[1024,1024]{1,0:T(8,128)(2,1)} fusion(bf16[1024,128]{1,0:T(8,128)(2,1)S(1)} %get-tuple-element.33, bf16[128,1024]{1,0:T(8,128)(2,1)S(1)} %copy-done), kind=kOutput, calls=%fused_computation.1 | convolution fusion | flops 269484032 | bytes 2621440 | tf_op jit(solution)/shard_map/dot_general | solution.py:746
  101.0 52.8 %reduce.7 = (bf16[2,128,1024]{2,1,0:T(8,128)(2,1)}, bf16[128,1024]{1,0:T(8,128)(2,1)}) custom-call(bf16[8,128,1024]{2,1,0:T(8,128)(2,1)} %bitcast.108, bf16[8,128,1024]{2,1,0:T(8,128)(2,1)} %bitcast.114, bf16[128,1024]{1,0:T(8,128)(2,1)} %convolution_convert_fusion.2.refs_2_), custom_call_target="tpu_custom_call" | custom-call | tf_op jit(solution)/shard_map/reduce/pallas_call | solution.py:755
  153.9 0.1 convert_reduce_fusion
  154.0 1.2 fusion.8
  155.2 1.2 fusion.13
  156.5 2.0 %fusion.12 = (bf16[1,128,1024]{2,1,0:T(8,128)(2,1)}, bf16[1,128,1024]{2,1,0:T(8,128)(2,1)}) fusion(bf16[1,128,1024]{2,1,0:T(8,128)(2,1)S(1)} %copy-done.2, bf16[1,128,1024]{2,1,0:T(8,128)(2,1)S(1)} %copy-done.5, f32[128]{0:T(128)S(1)} %negate_multiply_fusion, f32[128]{0:T(128)S(1)} %get-tuple-element.40, f32[128]{0:T(128)S(1)} %broadcast_multiply_fusion.2, ...), kind=kLoop, calls=%fused_computation.24 | loop fusion | flops 1966080 | bytes 1579008 | tf_op jit(solution)/shard_map/convert_element_type | solution.py:786
  158.5 0.8 convert_element_type.64
  (28 shorter events, 0.1 us)
Async XLA Ops:
  0.6 72.9 %copy-start = (bf16[128,1024]{1,0:T(8,128)(2,1)S(1)}, bf16[128,1024]{1,0:T(8,128)(2,1)}, u32[]{:S(2)}) copy-start(bf16[128,1024]{1,0:T(8,128)(2,1)} %param.14) | copy-start | bytes 786436
  2.1 2.3 %copy-start.9 = (s32[1,512]{1,0:T(1,128)S(1)}, s32[1,512]{1,0:T(1,128)}, u32[]{:S(2)}) copy-start(s32[1,512]{1,0:T(1,128)} %param.11) | copy-start | bytes 6148
  63.1 10.5 %copy-start.1 = (f32[2,4,128,512]{3,2,1,0:T(8,128)S(1)}, f32[2,4,128,512]{3,2,1,0:T(8,128)}, u32[]{:S(2)}) copy-start(f32[2,4,128,512]{3,2,1,0:T(8,128)} %get-tuple-element.13) | copy-start | bytes 6291460
  63.9 2.5 %copy-start.8 = (s32[2,4,128]{2,1,0:T(4,128)}, s32[2,4,128]{2,1,0:T(4,128)S(1)}, u32[]{:S(2)}) copy-start(s32[2,4,128]{2,1,0:T(4,128)S(1)} %slice.28) | copy-start | bytes 12292
  73.6 3.4 %copy-start.3 = (f32[2,512,128]{2,1,0:T(8,128)S(1)}, f32[2,512,128]{2,1,0:T(8,128)}, u32[]{:S(2)}) copy-start(f32[2,512,128]{2,1,0:T(8,128)} %get-tuple-element.14) | copy-start | bytes 1572868
  84.4 4.5 %copy-start.4 = (bf16[2,4,128,1024]{3,2,1,0:T(8,128)(2,1)S(1)}, bf16[2,4,128,1024]{3,2,1,0:T(8,128)(2,1)}, u32[]{:S(2)}) copy-start(bf16[2,4,128,1024]{3,2,1,0:T(8,128)(2,1)} %get-tuple-element.15) | copy-start | bytes 6291460
  90.0 5.2 %copy-start.10 = (bf16[8,128,512]{2,1,0:T(8,128)(2,1)S(1)}, bf16[8,128,512]{2,1,0:T(8,128)(2,1)}, u32[]{:S(2)}) copy-start(bf16[8,128,512]{2,1,0:T(8,128)(2,1)} %get-tuple-element.18) | copy-start | bytes 3145732
  101.0 52.9 %copy-start.2 = (bf16[1,128,1024]{2,1,0:T(8,128)(2,1)S(1)}, bf16[1,128,1024]{2,1,0:T(8,128)(2,1)}, u32[]{:S(2)}) copy-start(bf16[1,128,1024]{2,1,0:T(8,128)(2,1)} %param.9) | copy-start | bytes 786436
  101.0 53.0 %copy-start.7 = (f32[1024]{0:T(1024)S(1)}, f32[1024]{0:T(1024)}, u32[]{:S(2)}) copy-start(f32[1024]{0:T(1024)} %param.15) | copy-start | bytes 12292
  101.0 55.5 %copy-start.5 = (bf16[1,128,1024]{2,1,0:T(8,128)(2,1)S(1)}, bf16[1,128,1024]{2,1,0:T(8,128)(2,1)}, u32[]{:S(2)}) copy-start(bf16[1,128,1024]{2,1,0:T(8,128)(2,1)} %param.10) | copy-start | bytes 786436
  153.9 4.7 %copy-start.6 = (bf16[128,1024]{1,0:T(8,128)(2,1)S(1)}, bf16[128,1024]{1,0:T(8,128)(2,1)}, u32[]{:S(2)}) copy-start(bf16[128,1024]{1,0:T(8,128)(2,1)} %get-tuple-element.20) | copy-start | bytes 786436
where the time goes:
time: 160 us; the launch traced here: 159 us
  Pallas kernels  127 us (79%)
  other arithmetic  12.1 us (8%)
  matrix products  10.4 us (6%)
  local copies, waits for them, and re-layouts  7.9 us (5%)
    pallas_call x1, Pallas kernels, head_parallel(): pl.pallas_call(lambda *refs: gather_kernel(n_dp, n_seq, *refs), out_shape...  58 us
    pallas_call x1, Pallas kernels, head_parallel(): pl.pallas_call(lambda *refs: reduce_kernel(n_dp, n_seq, *refs), out_shape...  52.8 us
    pallas_call x1, Pallas kernels, head_parallel(): pl.pallas_call(lambda *refs: stats_kernel(n_dp, *refs), out_shape=sds((n_...  6.38 us
    pallas_call x1, Pallas kernels, head_parallel(): pl.pallas_call(backward_kernel, grid=(2,), out_shape=sds((2, seq_len, 4 *...  5.17 us
    pallas_call x1, Pallas kernels, head_parallel(): pl.pallas_call(forward_kernel, grid=(2,), out_shape=(sds((2, seq_len, DH)...  5.07 us
    dot_general x1, matrix products, head_parallel(): lax.dot_general(d_proj.reshape(count, 4 * DH), w_head, (((1,), (1,)), (()...  3.86 us
    dot_general x1, matrix products, head_parallel(): lax.dot_general(c_rows, w_out, (((1,), (1,)), ((), ())), preferred_elemen...  3.41 us

commit v1 on v0

v1 whole, which is shorter than its diff:
```python
import jax
import jax.numpy as jnp
from jax import lax
from jax.experimental import pallas as pl
from jax.experimental.pallas import tpu as pltpu
from jax.sharding import PartitionSpec as P

H = 8
DH = 128


EPS = 1e-05


def layer_norm(values, gain):
    average = jnp.mean(values, axis=-1, keepdims=True)
    centred = values - average
    variance = jnp.mean(centred * centred, axis=-1, keepdims=True)
    return centred * lax.rsqrt(variance + EPS) * gain


def silu_slope(values):
    sigmoid_v = jax.nn.sigmoid(values)
    return sigmoid_v * (1.0 + values * (1.0 - sigmoid_v))


def time_bias(bias_table, stamps_q, stamps_k):
    elapsed = stamps_q[:, None] - stamps_k[None, :]
    bucket = jnp.zeros(elapsed.shape, jnp.int32)
    for degree in range(1, bias_table.shape[1]):
        bucket = bucket + (elapsed >= 2**degree - 1).astype(jnp.int32)
    levels = jnp.arange(bias_table.shape[1], dtype=jnp.int32)
    one_hot = (bucket[:, :, None] == levels[None, None, :]).astype(jnp.float32)
    return jnp.einsum(
        "qkb,hb->hqk",
        one_hot,
        bias_table,
        precision=lax.Precision.HIGHEST,
        preferred_element_type=jnp.float32,
    )


def pair_terms(
    q_heads, d_heads, stamps_q, pos_q, k_heads, v_heads, stamps_k, pos_k, length, bias_table, scale
):
    scores = (
        jnp.einsum("qhd,khd->hqk", q_heads, k_heads, preferred_element_type=jnp.float32) * scale
    )
    scores = scores + time_bias(bias_table, stamps_q, stamps_k)
    allowed = (
        (pos_k[None, :] <= pos_q[:, None]) & (pos_k[None, :] < length) & (pos_q[:, None] < length)
    )
    weight = jnp.where(allowed[None], jax.nn.silu(scores), 0.0).astype(jnp.bfloat16)
    if d_heads is None:
        return (weight, None)
    d_weight = jnp.einsum("qhd,khd->hqk", d_heads, v_heads, preferred_element_type=jnp.float32)
    d_scores = jnp.where(allowed[None], d_weight * silu_slope(scores), 0.0).astype(jnp.bfloat16)
    return (weight, d_scores)


def per_device(tokens, cotangent, stamps, lengths, w_qkvu, w_out, gain_in, gain_out, bias_table):
    rows = tokens[0]
    cot_rows = cotangent[0]
    tok_count = rows.shape[0]
    feature_width = rows.shape[1]
    seq_count = lax.axis_size("seq")
    total_rows = tok_count * seq_count
    first_row = lax.axis_index("seq") * tok_count
    length = lengths[0]
    stamp_all = stamps[0]
    pos_own = first_row + jnp.arange(tok_count, dtype=jnp.int32)
    stamp_own = lax.dynamic_slice_in_dim(stamp_all, first_row, tok_count)
    scale = DH ** (-0.5)
    block_rows = min(512, total_rows)
    block_count = total_rows // block_rows
    w_full, w_out_full = (
        lax.all_gather(w_qkvu, "dp", axis=0, tiled=True),
        lax.all_gather(w_out, "dp", axis=0, tiled=True),
    )
    wide_rows = rows.astype(jnp.float32)
    normed = layer_norm(wide_rows, gain_in).astype(jnp.bfloat16)
    projected = jnp.dot(normed, w_full, preferred_element_type=jnp.float32)
    activated = jax.nn.silu(projected)
    gate_u = activated[:, :feature_width]
    values_own = activated[:, feature_width : 2 * feature_width].astype(jnp.bfloat16)
    queries_own = activated[:, 2 * feature_width : 3 * feature_width].astype(jnp.bfloat16)
    keys_own = activated[:, 3 * feature_width :].astype(jnp.bfloat16)
    keys_all, values_all = (
        lax.all_gather(keys_own, "seq", axis=0, tiled=True),
        lax.all_gather(values_own, "seq", axis=0, tiled=True),
    )
    q_heads = queries_own.reshape(tok_count, H, DH)

    def key_block(start):
        k_heads = lax.dynamic_slice_in_dim(keys_all, start, block_rows).reshape(block_rows, H, DH)
        v_heads = lax.dynamic_slice_in_dim(values_all, start, block_rows).reshape(block_rows, H, DH)
        stamps_k = lax.dynamic_slice_in_dim(stamp_all, start, block_rows)
        pos_k = start + jnp.arange(block_rows, dtype=jnp.int32)
        return (k_heads, v_heads, stamps_k, pos_k)

    def guarded(active, action, state):
        return lax.cond(active, action, lambda same: same, state)

    def reaches(start):
        return (start <= first_row + tok_count - 1) & (start < length) & (first_row < length)

    def forward_step(block_idx, totals):
        start = block_idx * block_rows

        def forward_compute(totals):
            k_heads, v_heads, stamps_k, pos_k = key_block(start)
            weight, unused = pair_terms(
                q_heads,
                None,
                stamp_own,
                pos_own,
                k_heads,
                v_heads,
                stamps_k,
                pos_k,
                length,
                bias_table,
                scale,
            )
            return totals + jnp.einsum(
                "hqk,khd->qhd", weight, v_heads, preferred_element_type=jnp.float32
            )

        return guarded(reaches(start), forward_compute, totals)

    attended = lax.fori_loop(
        0, block_count, forward_step, jnp.zeros((tok_count, H, DH), jnp.float32)
    )
    attended = attended.reshape(tok_count, feature_width)
    normed_att, norm_back = jax.vjp(lambda values: layer_norm(values, gain_out), attended)
    mixed_rows = (normed_att * gate_u).astype(jnp.bfloat16)
    mixed = (
        wide_rows + jnp.dot(mixed_rows, w_out_full, preferred_element_type=jnp.float32)
    ).astype(jnp.bfloat16)
    grad_part = lax.psum_scatter(
        jnp.einsum("tr,tc->rc", mixed_rows, cot_rows, preferred_element_type=jnp.float32).astype(
            jnp.bfloat16
        ),
        "dp",
        scatter_dimension=0,
        tiled=True,
    )
    w_grad = lax.psum(grad_part, "seq").astype(jnp.float32)
    d_mix = jnp.einsum("tc,rc->tr", cot_rows, w_out_full, preferred_element_type=jnp.float32)
    d_gate = d_mix * normed_att
    d_att = norm_back(d_mix * gate_u)[0].astype(jnp.bfloat16)
    d_heads = d_att.reshape(tok_count, H, DH)

    def backward_step():

        def step(block_idx, state_pair):
            start = block_idx * block_rows

            def step_compute(state_pair):
                q_grad, key_terms = state_pair
                k_heads, v_heads, stamps_k, pos_k = key_block(start)
                weight, d_scores = pair_terms(
                    q_heads,
                    d_heads,
                    stamp_own,
                    pos_own,
                    k_heads,
                    v_heads,
                    stamps_k,
                    pos_k,
                    length,
                    bias_table,
                    scale,
                )
                q_grad = (
                    q_grad
                    + jnp.einsum(
                        "hqk,khd->qhd", d_scores, k_heads, preferred_element_type=jnp.float32
                    )
                    * scale
                )
                k_grad = (
                    jnp.einsum(
                        "hqk,qhd->khd", d_scores, q_heads, preferred_element_type=jnp.float32
                    )
                    * scale
                )
                v_grad = jnp.einsum(
                    "hqk,qhd->khd", weight, d_heads, preferred_element_type=jnp.float32
                )
                joined = jnp.concatenate(
                    [
                        k_grad.reshape(block_rows, feature_width),
                        v_grad.reshape(block_rows, feature_width),
                    ],
                    axis=1,
                )
                key_terms = lax.dynamic_update_slice_in_dim(key_terms, joined, start, 0)
                return (q_grad, key_terms)

            return guarded(reaches(start), step_compute, state_pair)

        return step

    q_start = jnp.zeros((tok_count, H, DH), jnp.float32)
    term_start = jnp.zeros((total_rows, 2 * feature_width), jnp.float32)
    q_grad, key_terms = lax.fori_loop(0, block_count, backward_step(), (q_start, term_start))
    key_grads = lax.psum_scatter(
        key_terms.astype(jnp.bfloat16), "seq", scatter_dimension=0, tiled=True
    ).astype(jnp.float32)
    d_act = jnp.concatenate(
        [
            d_gate,
            key_grads[:, feature_width:],
            q_grad.reshape(tok_count, feature_width),
            key_grads[:, :feature_width],
        ],
        axis=1,
    )
    d_proj = (d_act * silu_slope(projected)).astype(jnp.bfloat16)
    d_normed = jnp.einsum("tf,df->td", d_proj, w_full, preferred_element_type=jnp.float32)
    unused_rows, in_back = jax.vjp(lambda values: layer_norm(values, gain_in), wide_rows)
    input_grad = (cot_rows.astype(jnp.float32) + in_back(d_normed)[0]).astype(jnp.bfloat16)
    return (mixed[None], input_grad[None], w_grad)


MESH = pl.DeviceIdType.MESH
VM = pl.BlockSpec(memory_space=pltpu.VMEM)
F32 = jnp.float32
BF16 = jnp.bfloat16
MASKED = -1e30


def mm(a, b, dims):
    return lax.dot_general(a, b, (dims, ((), ())), preferred_element_type=F32)


def remote(src, dst, send_sem, recv_sem, target):
    return pltpu.make_async_remote_copy(
        src_ref=src,
        dst_ref=dst,
        send_sem=send_sem,
        recv_sem=recv_sem,
        device_id=target,
        device_id_type=MESH,
    )


def arrived(dst, sem):
    pltpu.make_async_copy(dst, dst, sem).wait()


def column_kernel(
    n_dp, n_seq, w_ref, x_ref, c_ref, wo_ref, meta_ref, gin_ref, gout_ref, bias_ref,
    mixed_ref, grad_ref, wg_ref,
    W, X, C, WO, mbuf, NB, BI, PJ, GT, ACT, ATT, WT, SL, DM, DG, DA, DP, MR, KA, VA, ST,
    MW, WG, PS, PR, TS, TR, PB, SB, CS, FB, FIN, RO,
    wsend, wrelay, wrecv, zsend, ssend, farsend, xrecv, wosend, worecv, msem,
    stsend, strecv, gsend, grecv, hsem, tsend, trecv, psend, precv, csend, crecv, osend, orecv,
):
    me = lax.axis_index("dp")
    z = lax.axis_index("seq")
    tok, width = x_ref.shape
    rows = tok * n_seq
    half = tok // 2
    n_heads = n_dp
    scale = DH ** (-0.5)
    chip, k = me // 2, me % 2
    cy, cx = chip // 2, chip % 2
    xn, yn = 2 * cy + (1 - cx), 2 * (1 - cy) + cx
    dn = 2 * (1 - cy) + (1 - cx)
    sib = 2 * chip + (1 - k)
    p, ks = z % 2, z // 2
    near, far = 1 + ks, (n_seq - 1) * ks
    zp = near + far - z
    is_near, is_far = z == near, z == far
    is_main = k == ks
    is_aux = jnp.logical_not(is_main)
    main_dp = 2 * chip + ks

    def head_of(core, j):
        return 4 * core + 2 * j + p

    def rows_of(ref_rows, index):
        return pl.ds(pl.multiple_of(index * ref_rows, ref_rows), ref_rows)

    def lanes_of(index):
        return pl.ds(pl.multiple_of(index * DH, DH), DH)

    def w_copies(core, j, make):
        return [
            make(
                w_ref.at[:, lanes_of(g * n_heads + head_of(core, j))],
                W.at[j, rows_of(tok, me), slice(g * DH, (g + 1) * DH)],
            )
            for g in range(4)
        ]

    w_targets = ((xn, 0, 1), (yn, 1, 4), (chip, 1 - k, 0), (xn, 1, 2), (yn, 0, 3))

    def w_start(j):
        for where, core, index in w_targets:
            for copy in w_copies(
                core, j,
                lambda s, d: remote(s, d, wsend.at[index, j], wrecv.at[me, j], (2 * where + core, z)),
            ):
                copy.start()

    def w_piece(src, j):
        return W.at[j, rows_of(tok, src)]

    via, to = (1 - k) * xn + k * yn, (1 - k) * yn + k * xn

    def w_relay(i, j):
        src = 2 * via + i
        block = w_piece(src, j)
        return remote(block, block, wrelay.at[i, j], wrecv.at[src, j], (2 * to + k, z))

    def w_wait(src, j):
        arrived(w_piece(src, j), wrecv.at[src, j])

    ins, outs = (x_ref, c_ref), (X, C)
    z_to = jnp.where(is_main, zp, 1 + k)

    def z_send(a):
        return remote(ins[a], outs[a].at[z], zsend.at[a], xrecv.at[a, z], (me, z_to))

    def own_copy(a):
        return pltpu.make_async_copy(ins[a], outs[a].at[z], xrecv.at[a, z])

    def share(a, b):
        block = ins[a] if b is None else outs[a].at[b]
        at = z if b is None else b
        return remote(block, outs[a].at[at], ssend.at[a, at], xrecv.at[a, at], (sib, z))

    foreign = (2 * (1 - ks), 2 * (1 - ks) + 1)

    def to_far(a, i):
        block = outs[a].at[foreign[i]]
        return remote(block, block, farsend.at[a, i], xrecv.at[a, foreign[i]], (me, far))

    def x_wait(a, b):
        arrived(outs[a].at[b], xrecv.at[a, b])

    def meta_send():
        return remote(meta_ref, mbuf, msem.at[0], msem.at[1], (sib, z))

    wo_core, wo_slot = chip // 2, chip % 2
    wo_here = wo_core == k
    wo_sends = [
        remote(wo_ref, WO.at[wo_slot], wosend.at[i], worecv.at[wo_slot], (2 * where + wo_core, z))
        for i, where in enumerate((xn, yn, dn, chip))
    ]

    @pl.when(is_main)
    def _():
        pltpu.make_async_copy(meta_ref, mbuf, msem.at[1]).start()
        meta_send().start()

    w_start(0)
    z_send(0).start()

    @pl.when(is_main)
    def _():
        own_copy(0).start()
        share(0, None).start()

    z_send(1).start()

    @pl.when(is_main)
    def _():
        own_copy(1).start()
        share(1, None).start()

    for j in range(2):
        for copy in w_copies(k, j, lambda s, d: pltpu.make_async_copy(s, d, wrecv.at[me, j])):
            copy.start()

    def relay_weights(j):
        for i in range(2):
            w_wait(2 * via + i, j)
            w_relay(i, j).start()

    def near_relay(a):
        @pl.when(is_main)
        def _():
            x_wait(a, zp)
            share(a, zp).start()

        @pl.when(is_main & is_near)
        def _():
            for i in range(2):
                x_wait(a, foreign[i])
                to_far(a, i).start()
                share(a, foreign[i]).start()

    def far_relay(a):
        @pl.when(is_main & is_far)
        def _():
            for i in range(2):
                x_wait(a, foreign[i])
                share(a, foreign[i]).start()

    relay_weights(0)
    w_start(1)
    near_relay(0)

    arrived(mbuf, msem.at[1])
    lane_row = lax.broadcasted_iota(jnp.int32, (DH, DH), 0)
    lane_col = lax.broadcasted_iota(jnp.int32, (DH, DH), 1)
    length = mbuf[n_seq : n_seq + 1, :]
    for i in range(n_seq):
        col = jnp.broadcast_to(mbuf[i : i + 1, :].astype(F32), (DH, DH)).T
        valid = lane_row + i * DH < length
        for b in range(i + 1):
            elapsed = col - mbuf[b : b + 1, :].astype(F32)
            allowed = valid & (lane_col <= lane_row) if b == i else valid
            heads = [head_of(k, j) for j in range(2)]
            terms = [jnp.full(elapsed.shape, bias_ref[h, 0], F32) for h in heads]
            for degree in range(1, bias_ref.shape[1]):
                reached = elapsed >= float(2**degree - 1)
                terms = [
                    jnp.where(reached, bias_ref[h, degree], t) for h, t in zip(heads, terms)
                ]
            for j in range(2):
                BI[j, i * DH : (i + 1) * DH, b * DH : (b + 1) * DH] = jnp.where(
                    allowed, terms[j], MASKED
                )

    relay_weights(1)

    @pl.when(k == p)
    def _():
        for i in range(3):
            wo_sends[i].start()

        @pl.when(wo_here)
        def _():
            pltpu.make_async_copy(wo_ref, WO.at[wo_slot], worecv.at[wo_slot]).start()

        @pl.when(jnp.logical_not(wo_here))
        def _():
            wo_sends[3].start()

    far_relay(0)
    near_relay(1)

    @pl.when(is_main)
    def _():
        x_wait(0, z)

    @pl.when(is_aux)
    def _():
        for b in range(n_seq):
            x_wait(0, b)

    for b in range(n_seq):
        NB[b * tok : (b + 1) * tok, :] = layer_norm(X[b].astype(F32), gin_ref[...]).astype(BF16)

    def forward(j):
        w_wait(me, j)
        w_wait(sib, j)
        for i in range(2):
            w_wait(2 * to + i, j)
            w_wait(2 * dn + i, j)
        PJ[j] = mm(NB[...], W[j], ((1,), (0,)))
        cols = slice(j * DH, (j + 1) * DH)
        GT[:, cols] = jax.nn.silu(PJ[j, :, :DH])
        for g in range(3):
            ACT[j, g] = jax.nn.silu(PJ[j, :, (1 + g) * DH : (2 + g) * DH]).astype(BF16)
        for i in range(n_seq):
            at, end = slice(i * tok, (i + 1) * tok), (i + 1) * tok
            scores = mm(ACT[j, 1, at], ACT[j, 2, :end], ((1,), (1,))) * scale + BI[j, at, :end]
            sig = jax.nn.sigmoid(scores)
            weight = (scores * sig).astype(BF16)
            WT[j, at, :end] = weight
            SL[j, at, :end] = sig * (1.0 + scores * (1.0 - sig))
            ATT[at, cols] = mm(weight, ACT[j, 0, :end], ((1,), (0,)))

    forward(0)
    far_relay(1)
    forward(1)

    @pl.when(is_main)
    def _():
        x_wait(1, z)

    @pl.when(is_aux)
    def _():
        for b in range(n_seq):
            x_wait(1, b)

    for j in range(2):
        arrived(WO.at[j], worecv.at[j])
    wo_heads = WO[...].reshape(2 * DH, width)
    c_rows = C[...].reshape(rows, width)
    DM[...] = mm(c_rows, wo_heads, ((1,), (1,)))

    gain = jnp.concatenate([gout_ref[:, lanes_of(head_of(k, j))] for j in range(2)], axis=1)
    pid = 2 * p + k
    own_width = 2 * DH
    for b in range(n_seq):
        at = slice(b * tok, (b + 1) * tok)
        att = ATT[at, :]
        g = DM[at, :] * GT[at, :] * gain
        mean_own = jnp.mean(att, axis=1, keepdims=True)
        off = att - mean_own
        packed = jnp.where(
            lane_col == 0,
            mean_own,
            jnp.where(
                lane_col == 1,
                jnp.sum(off * off, axis=1, keepdims=True),
                jnp.where(
                    lane_col == 2,
                    jnp.sum(g, axis=1, keepdims=True),
                    jnp.sum(g * off, axis=1, keepdims=True),
                ),
            ),
        )
        ST[pid, :, at] = packed.T[:8]
    st_peers = ((sib, z), (me, zp), (sib, zp))
    st_slots = (2 * p + 1 - k, 2 * (1 - p) + k, 2 * (1 - p) + 1 - k)
    st_sends = [
        remote(ST.at[pid], ST.at[pid], stsend.at[i], strecv.at[pid], peer)
        for i, peer in enumerate(st_peers)
    ]
    for copy in st_sends:
        copy.start()
    for slot in st_slots:
        arrived(ST.at[slot], strecv.at[slot])
    means = [ST[q, 0:1, :] for q in range(4)]
    mean = sum(means[1:], means[0]) / 4.0
    shifts = [m - mean for m in means]
    squares = sum(ST[q, 1:2, :] + own_width * shifts[q] * shifts[q] for q in range(4))
    rstd = lax.rsqrt(squares / width + EPS)
    g_mean = sum(ST[q, 2:3, :] for q in range(4)) / width
    g_dot = rstd * sum(ST[q, 3:4, :] + shifts[q] * ST[q, 2:3, :] for q in range(4)) / width
    table = jnp.concatenate([mean, rstd, g_mean, g_dot, mean, rstd, g_mean, g_dot], axis=0)
    for b in range(n_seq):
        at = slice(b * tok, (b + 1) * tok)
        turned = jnp.concatenate([table[:, at]] * (DH // 8), axis=0).T
        mean_c, rstd_c, g_mean_c, g_dot_c = [turned[:, q : q + 1] for q in range(4)]
        d_mix, gate = DM[at, :], GT[at, :]
        hat = (ATT[at, :] - mean_c) * rstd_c
        normed_att = hat * gain
        MR[at, :] = (normed_att * gate).astype(BF16)
        DG[at, :] = d_mix * normed_att
        DA[at, :] = (rstd_c * (d_mix * gate * gain - g_mean_c - hat * g_dot_c)).astype(BF16)

    def block_at(i):
        return (1 - ks) * (n_seq - 1 - i) + ks * i

    def pair_send(o, i):
        return remote(PB.at[o, i, 1 - k], SB.at[o, i], psend.at[o, i], precv.at[o, i], (sib, z))

    def cross_send(o, i):
        return remote(CS.at[o, i], FB.at[o, i], csend.at[o, i], crecv.at[o, i], (me, zp))

    def home_is_self(i):
        return is_main & (block_at(i) == z)

    def home_send(o, i):
        return remote(
            FIN.at[o, i], RO.at[o, k], osend.at[o, i], orecv.at[o, k], (main_dp, block_at(i))
        )

    last = n_seq - 1

    def sends_cross(i):
        return is_near if i == last else is_far

    def put_partial(o, i, part):
        PB[o, i, 0] = part[:half].astype(BF16)
        PB[o, i, 1] = part[half:].astype(BF16)

    def pair_sum(o, i):
        return PB[o, i, k].astype(F32) + SB[o, i].astype(F32)

    def cross(o):
        for i in range(n_seq):
            arrived(SB.at[o, i], precv.at[o, i])

            @pl.when(sends_cross(i))
            def _():
                CS[o, i] = pair_sum(o, i).astype(BF16)
                cross_send(o, i).start()

    def finish(o):
        for i in range(n_seq):

            @pl.when(jnp.logical_not(sends_cross(i)))
            def _():
                arrived(FB.at[o, i], crecv.at[o, i])
                FIN[o, i] = (pair_sum(o, i) + FB[o, i].astype(F32)).astype(BF16)
                if i < 2:
                    home_send(o, i).start()
                else:

                    @pl.when(home_is_self(i))
                    def _():
                        pltpu.make_async_copy(FIN.at[o, i], RO.at[o, k], orecv.at[o, k]).start()

                    @pl.when(jnp.logical_not(home_is_self(i)))
                    def _():
                        home_send(o, i).start()

    for i in range(n_seq):
        put_partial(0, i, mm(MR[rows_of(tok, block_at(i)), :], wo_heads, ((1,), (0,))))
        if i > 0:
            pair_send(0, i - 1).start()
    pair_send(0, last).start()

    def g_send(j):
        return remote(MW.at[j], WG.at[chip], gsend.at[j], grecv.at[chip], (2 * (2 * k + j) + p, z))

    def g_self(j):
        return (2 * k + j == chip) & (k == p)

    for j in range(2):
        MW[j] = mm(MR[:, j * DH : (j + 1) * DH], c_rows, ((0,), (0,))).astype(BF16)
    cross(0)
    for j in range(2):

        @pl.when(g_self(j))
        def _():
            pltpu.make_async_copy(MW.at[j], WG.at[chip], grecv.at[chip]).start()

        @pl.when(jnp.logical_not(g_self(j)))
        def _():
            g_send(j).start()

    is_root = k == p
    centre = 2 - k
    is_centre = z == centre

    def h_send():
        return remote(PS, PR, hsem.at[0], hsem.at[1], (me, lax.rem(z + 2, n_seq)))

    def t_send(i):
        return remote(TS, TR, tsend.at[i], trecv, (me, z - 1 + 2 * i))

    def plane_sum():
        @pl.when(is_root)
        def _():
            for c in range(n_dp // 2):
                arrived(WG.at[c], grecv.at[c])
            total = WG[0].astype(F32)
            for c in range(1, n_dp // 2):
                total = total + WG[c].astype(F32)
            PS[...] = total.astype(BF16)
            h_send().start()

    def plane_total():
        @pl.when(is_root)
        def _():
            arrived(PR, hsem.at[1])
            TS[...] = (PS[...].astype(F32) + PR[...].astype(F32)).astype(BF16)
            wg_ref[...] = TS[...].astype(F32)

            @pl.when(is_centre)
            def _():
                for i in range(2):
                    t_send(i).start()

    def backward(j):
        values, queries, keys = [ACT[j, g] for g in range(3)]
        cols = slice(j * DH, (j + 1) * DH)

        def put(group, start, end, grad):
            at = slice(group * DH, (group + 1) * DH)
            DP[j, start:end, at] = (grad * silu_slope(PJ[j, start:end, at])).astype(BF16)

        for i in reversed(range(n_seq)):
            start, end = i * tok, (i + 1) * tok
            d_att = DA[start:end, cols]
            d_weight = mm(d_att, values[:end], ((1,), (1,)))
            d_scores = (d_weight * SL[j, start:end, :end]).astype(BF16)
            put(2, start, end, mm(d_scores, keys[:end], ((1,), (0,))) * scale)
            k_part = mm(d_scores, queries[start:end], ((0,), (0,)))
            v_part = mm(WT[j, start:end, :end], d_att, ((0,), (0,)))
            if end == rows:
                KA[...] = k_part
                VA[...] = v_part
            else:
                KA[:end] += k_part
                VA[:end] += v_part
        put(0, 0, rows, DG[:, cols])
        put(1, 0, rows, VA[...])
        put(3, 0, rows, KA[...] * scale)

    backward(0)
    finish(0)
    plane_sum()
    backward(1)
    for i in range(n_seq):
        at = rows_of(tok, block_at(i))
        put_partial(
            1, i, mm(DP[0, at, :], W[0], ((1,), (1,))) + mm(DP[1, at, :], W[1], ((1,), (1,)))
        )
        if i > 0:
            pair_send(1, i - 1).start()
    pair_send(1, last).start()
    cross(1)
    plane_total()
    finish(1)

    for h in range(2):
        arrived(RO.at[0, h], orecv.at[0, h])
    wide = x_ref[...].astype(F32)
    mixed_ref[...] = (wide + RO[0].reshape(tok, width).astype(F32)).astype(BF16)

    @pl.when(jnp.logical_not(is_root))
    def _():
        arrived(TR, trecv)
        wg_ref[...] = TR[...].astype(F32)

    average = jnp.mean(wide, axis=-1, keepdims=True)
    centred = wide - average
    inv = lax.rsqrt(jnp.mean(centred * centred, axis=-1, keepdims=True) + EPS)
    hat = centred * inv
    for h in range(2):
        arrived(RO.at[1, h], orecv.at[1, h])
    grad = RO[1].reshape(tok, width).astype(F32) * gin_ref[...]
    back = inv * (
        grad
        - jnp.mean(grad, axis=-1, keepdims=True)
        - hat * jnp.mean(grad * hat, axis=-1, keepdims=True)
    )
    grad_ref[...] = (c_ref[...].astype(F32) + back).astype(BF16)

    for j in range(2):
        for index in range(5):
            block = w_piece(me, j)
            remote(block, block, wsend.at[index, j], wrecv.at[me, j], (sib, z)).wait_send()
        for i in range(2):
            w_relay(i, j).wait_send()

        @pl.when(jnp.logical_not(g_self(j)))
        def _():
            g_send(j).wait_send()

    for a in range(2):
        z_send(a).wait_send()

        @pl.when(is_main)
        def _():
            share(a, None).wait_send()
            share(a, zp).wait_send()
            for i in range(2):
                share(a, foreign[i]).wait_send()

        @pl.when(is_main & is_near)
        def _():
            for i in range(2):
                to_far(a, i).wait_send()

    @pl.when(is_main)
    def _():
        meta_send().wait_send()

    @pl.when(k == p)
    def _():
        for i in range(3):
            wo_sends[i].wait_send()

        @pl.when(jnp.logical_not(wo_here))
        def _():
            wo_sends[3].wait_send()

    for copy in st_sends:
        copy.wait_send()

    @pl.when(is_root)
    def _():
        h_send().wait_send()

        @pl.when(is_centre)
        def _():
            for i in range(2):
                t_send(i).wait_send()

    for o in range(2):
        for i in range(n_seq):
            pair_send(o, i).wait_send()

            @pl.when(sends_cross(i))
            def _():
                cross_send(o, i).wait_send()

            @pl.when(jnp.logical_not(sends_cross(i)) & jnp.logical_not(home_is_self(i)))
            def _():
                home_send(o, i).wait_send()


def column_parallel(
    n_dp, n_seq, tokens, cotangent, stamps, lengths, w_qkvu, w_out, gain_in, gain_out, bias_table
):
    tok, width = tokens.shape[1:]
    rows = tok * n_seq
    meta = jnp.concatenate([stamps.reshape(-1, DH), jnp.broadcast_to(lengths[:, None], (4, DH))])
    dma = pltpu.SemaphoreType.DMA
    sds = jax.ShapeDtypeStruct
    smem = pl.BlockSpec(memory_space=pltpu.SMEM)

    def vb(*shape):
        return pltpu.VMEM(shape, BF16)

    def vf(*shape):
        return pltpu.VMEM(shape, F32)

    half = tok // 2
    mixed, grad, w_grad = pl.pallas_call(
        lambda *refs: column_kernel(n_dp, n_seq, *refs),
        out_shape=(sds((tok, width), BF16), sds((tok, width), BF16), sds(w_out.shape, F32)),
        in_specs=[VM] * 7 + [smem],
        out_specs=[VM] * 3,
        scratch_shapes=[
            vb(2, width, 4 * DH),
            vb(n_seq, tok, width),
            vb(n_seq, tok, width),
            vb(2, DH, width),
            pltpu.VMEM(meta.shape, jnp.int32),
            vb(rows, width),
            vf(2, rows, rows),
            vf(2, rows, 4 * DH),
            vf(rows, 2 * DH),
            vb(2, 3, rows, DH),
            vf(rows, 2 * DH),
            vb(2, rows, rows),
            vf(2, rows, rows),
            vf(rows, 2 * DH),
            vf(rows, 2 * DH),
            vb(rows, 2 * DH),
            vb(2, rows, 4 * DH),
            vb(rows, 2 * DH),
            vf(rows, DH),
            vf(rows, DH),
            vf(4, 8, rows),
            vb(2, DH, width),
            vb(n_dp // 2, DH, width),
            vb(DH, width),
            vb(DH, width),
            vb(DH, width),
            vb(DH, width),
            vb(2, n_seq, 2, half, width),
            vb(2, n_seq, half, width),
            vb(2, n_seq, half, width),
            vb(2, n_seq, half, width),
            vb(2, n_seq, half, width),
            vb(2, 2, half, width),
            dma((5, 2)),
            dma((2, 2)),
            dma((n_dp, 2)),
            dma((2,)),
            dma((2, n_seq)),
            dma((2, 2)),
            dma((2, n_seq)),
            dma((4,)),
            dma((2,)),
            dma((2,)),
            dma((3,)),
            dma((4,)),
            dma((2,)),
            dma((n_dp // 2,)),
            dma((2,)),
            dma((2,)),
            dma,
            dma((2, n_seq)),
            dma((2, n_seq)),
            dma((2, n_seq)),
            dma((2, n_seq)),
            dma((2, n_seq)),
            dma((2, 2)),
        ],
        compiler_params=pltpu.CompilerParams(has_side_effects=True),
        name="column",
    )(
        w_qkvu, tokens[0], cotangent[0], w_out, meta, gain_in[None], gain_out[None], bias_table
    )
    return (mixed[None], grad[None], w_grad)


def solution(mesh):
    n_dp, n_seq = mesh.shape["dp"], mesh.shape["seq"]

    def body(*args):
        tokens, stamps, w_out = args[0], args[2], args[5]
        mesh_fits = n_seq == 4 and n_dp == 2 * n_seq and n_dp == H
        sizes_fit = w_out.shape[0] == DH and tokens.shape[1] == DH
        if mesh_fits and sizes_fit and stamps.shape == (1, n_seq * DH):
            return column_parallel(n_dp, n_seq, *args)
        return per_device(*args)

    return jax.shard_map(
        body,
        mesh=mesh,
        in_specs=(
            P("dp", "seq", None),
            P("dp", "seq", None),
            P("dp", None),
            P("dp"),
            P("dp", None),
            P("dp", None),
            P(),
            P(),
            P(),
        ),
        out_specs=(P("dp", "seq", None), P("dp", "seq", None), P("dp", None)),
        check_vma=False,
    )
```

time: 160 us -> 75.6 us (0.47)
  the two profiles are of different devices: /device:TPU:3 before, /device:TPU:1 now
where the time goes in v1:
time: 75.6 us; the launch traced here: 75.4 us
  Pallas kernels  69.6 us (92%)
  local copies, waits for them, and re-layouts  4.51 us (6%)
  between operations  1.31 us (2%)
    pallas_call x1, Pallas kernels, column_parallel(): pl.pallas_call(lambda *refs: column_kernel(n_dp, n_seq, *refs), out_shape...  69.6 us
    unnamed x9, local copies, waits for them, and re-layouts  3.92 us

profile of v1, /device:TPU:1, one launch (start us, length us, event | category | flops | bytes accessed | tf_op | source)
XLA Modules:
  0.0 75.4 jit_solution(4242319179517003692)
XLA Ops:
  1.3 0.0 copy-start.2
  1.3 0.7 copy-done.2
  2.0 0.6 concatenate.3.refs_4_
  2.6 69.6 %column.1 = (bf16[128,1024]{1,0:T(8,128)(2,1)}, bf16[128,1024]{1,0:T(8,128)(2,1)}, f32[128,1024]{1,0:T(8,128)}) custom-call(bf16[128,4096]{1,0:T(8,128)(2,1)} %refs_0_.1, bf16[128,1024]{1,0:T(8,128)(2,1)} %bitcast.9, bf16[128,1024]{1,0:T(8,128)(2,1)} %bitcast.10, bf16[128,1024]{1,0:T(8,128)(2,1)} %refs_3_.1, s32[8,128]{1,0:T(8,128)} %concatenate.3.refs_4_, ...), custom_call_target="tpu_custom_call" | custom-call | tf_op jit(solution)/shard_map/column/pallas_call | solution.py:813
  72.1 0.0 copy-start.1
  72.1 0.0 copy-start
  72.2 1.7 %copy.16 = bf16[1,128,1024]{2,1,0:T(8,128)(2,1)} copy(bf16[1,128,1024]{2,1,0:T(8,128)(2,1)} %bitcast.12) | data formatting | bytes 524288
  73.9 0.0 copy-done.1
  73.9 0.7 copy.17
  74.6 0.0 copy-done
  74.6 0.8 %copy.18 = f32[128,1024]{1,0:T(8,128)} copy(f32[128,1024]{1,0:T(8,128)S(1)} %copy-done) | data formatting | bytes 1048576
Async XLA Ops:
  1.3 0.7 copy-start.2
  72.1 1.8 %copy-start.1 = (bf16[128,1024]{1,0:T(8,128)(2,1)S(1)}, bf16[128,1024]{1,0:T(8,128)(2,1)}, u32[]{:S(2)}) copy-start(bf16[128,1024]{1,0:T(8,128)(2,1)} %get-tuple-element.7) | copy-start | bytes 786436
  72.1 2.5 %copy-start = (f32[128,1024]{1,0:T(8,128)S(1)}, f32[128,1024]{1,0:T(8,128)}, u32[]{:S(2)}) copy-start(f32[128,1024]{1,0:T(8,128)} %get-tuple-element.14) | copy-start | bytes 1572868

commit v2 on v1

--- a/solution.py
+++ b/solution.py
@@ -251,12 +251,13 @@
 
 
 def column_kernel(
-    n_dp, n_seq, w_ref, x_ref, c_ref, wo_ref, meta_ref, gin_ref, gout_ref, bias_ref,
+    n_dp, n_seq, w_hbm, x_hbm, c_hbm, wo_hbm, stamps_hbm, length_ref, gin_hbm, gout_hbm, bias_hbm,
     mixed_ref, grad_ref, wg_ref,
-    W, X, C, WO, mbuf, NB, BI, PJ, GT, ACT, ATT, WT, SL, DM, DG, DA, DP, MR, KA, VA, ST,
-    MW, WG, PS, PR, TS, TR, PB, SB, CS, FB, FIN, RO,
-    wsend, wrelay, wrecv, zsend, ssend, farsend, xrecv, wosend, worecv, msem,
-    stsend, strecv, gsend, grecv, hsem, tsend, trecv, psend, precv, csend, crecv, osend, orecv,
+    w_ref, x_ref, c_ref, wo_ref, stamps_ref, gin_ref, gout_ref, bias_ref, meta_ref,
+    W, X, C, WO, mbuf, NB, BI, PJ, GT, ACT, ATT, WT, SL, DM, DG, DA, DP, MR, KA, VA, SA, SG, TB,
+    MW, WG, PS, PR, TS, TR, MA, MB, PB, SB, CS, FB, FIN, RO,
+    lsem, wsend, wrelay, wrecv, zsend, ssend, farsend, xrecv, wosend, worecv, msem,
+    sasend, sarecv, sgsend, sgrecv, gsend, grecv, hsem, tsend, trecv, psend, precv, csend, crecv, osend, orecv,
 ):
     me = lax.axis_index("dp")
     z = lax.axis_index("seq")
@@ -352,6 +353,29 @@
         for i, where in enumerate((xn, yn, dn, chip))
     ]
 
+    loads = [
+        pltpu.make_async_copy(src, dst, lsem.at[i])
+        for i, (src, dst) in enumerate(
+            (
+                (stamps_hbm, stamps_ref), (w_hbm, w_ref), (x_hbm, x_ref), (c_hbm, c_ref),
+                (wo_hbm, wo_ref), (gin_hbm, gin_ref), (gout_hbm, gout_ref), (bias_hbm, bias_ref),
+            )
+        )
+    ]
+    barrier = pltpu.get_barrier_semaphore()
+    peers = [(lax.rem(me + step, n_dp), z) for step in range(1, n_dp)]
+    for step in range(1, n_seq):
+        peers += [(me, lax.rem(z + step, n_seq)), (sib, lax.rem(z + step, n_seq))]
+    for peer in peers:
+        pl.semaphore_signal(barrier, inc=1, device_id=peer, device_id_type=MESH)
+    for load in loads:
+        load.start()
+    loads[0].wait()
+    meta_ref[0:1, :] = stamps_ref[...]
+    meta_ref[1:2, :] = jnp.full(stamps_ref.shape, length_ref[0], jnp.int32)
+    for load in loads[1:]:
+        load.wait()
+    pl.semaphore_wait(barrier, len(peers))
     @pl.when(is_main)
     def _():
         pltpu.make_async_copy(meta_ref, mbuf, msem.at[1]).start()
@@ -408,12 +432,12 @@
     arrived(mbuf, msem.at[1])
     lane_row = lax.broadcasted_iota(jnp.int32, (DH, DH), 0)
     lane_col = lax.broadcasted_iota(jnp.int32, (DH, DH), 1)
-    length = mbuf[n_seq : n_seq + 1, :]
+    length = mbuf[1:2, :DH]
     for i in range(n_seq):
-        col = jnp.broadcast_to(mbuf[i : i + 1, :].astype(F32), (DH, DH)).T
+        col = jnp.broadcast_to(mbuf[0:1, i * DH : (i + 1) * DH].astype(F32), (DH, DH)).T
         valid = lane_row + i * DH < length
         for b in range(i + 1):
-            elapsed = col - mbuf[b : b + 1, :].astype(F32)
+            elapsed = col - mbuf[0:1, b * DH : (b + 1) * DH].astype(F32)
             allowed = valid & (lane_col <= lane_row) if b == i else valid
             heads = [head_of(k, j) for j in range(2)]
             terms = [jnp.full(elapsed.shape, bias_ref[h, 0], F32) for h in heads]
@@ -427,6 +451,7 @@
                     allowed, terms[j], MASKED
                 )
 
+    near_relay(1)
     relay_weights(1)
 
     @pl.when(k == p)
@@ -443,7 +468,6 @@
             wo_sends[3].start()
 
     far_relay(0)
-    near_relay(1)
 
     @pl.when(is_main)
     def _():
@@ -478,75 +502,67 @@
             ATT[at, cols] = mm(weight, ACT[j, 0, :end], ((1,), (0,)))
 
     forward(0)
+    forward(1)
+
+    gain = jnp.concatenate([gout_ref[:, lanes_of(head_of(k, j))] for j in range(2)], axis=1)
+    pid = 2 * p + k
+    own_width = 2 * DH
+    st_peers = ((sib, z), (me, zp), (sib, zp))
+    st_slots = (2 * p + 1 - k, 2 * (1 - p) + k, 2 * (1 - p) + 1 - k)
+
+    def stat_sends(ref, send_sem, recv_sem):
+        return [
+            remote(ref.at[pid], ref.at[pid], send_sem.at[i], recv_sem.at[pid], peer)
+            for i, peer in enumerate(st_peers)
+        ]
+
+    def put_stats(ref, at, first, second):
+        ref[pid, :, at] = jnp.where(lane_col == 0, first, second).T[:8]
+
+    for b in range(n_seq):
+        at = slice(b * tok, (b + 1) * tok)
+        att = ATT[at, :]
+        mean_own = jnp.mean(att, axis=1, keepdims=True)
+        off = att - mean_own
+        put_stats(SA, at, mean_own, jnp.sum(off * off, axis=1, keepdims=True))
+    for copy in stat_sends(SA, sasend, sarecv):
+        copy.start()
     far_relay(1)
-    forward(1)
-
-    @pl.when(is_main)
-    def _():
-        x_wait(1, z)
-
-    @pl.when(is_aux)
-    def _():
-        for b in range(n_seq):
-            x_wait(1, b)
-
     for j in range(2):
         arrived(WO.at[j], worecv.at[j])
     wo_heads = WO[...].reshape(2 * DH, width)
+    @pl.when(is_main)
+    def _():
+        x_wait(1, z)
+
+    @pl.when(is_aux)
+    def _():
+        for b in range(n_seq):
+            x_wait(1, b)
+
     c_rows = C[...].reshape(rows, width)
     DM[...] = mm(c_rows, wo_heads, ((1,), (1,)))
-
-    gain = jnp.concatenate([gout_ref[:, lanes_of(head_of(k, j))] for j in range(2)], axis=1)
-    pid = 2 * p + k
-    own_width = 2 * DH
     for b in range(n_seq):
         at = slice(b * tok, (b + 1) * tok)
         att = ATT[at, :]
         g = DM[at, :] * GT[at, :] * gain
-        mean_own = jnp.mean(att, axis=1, keepdims=True)
-        off = att - mean_own
-        packed = jnp.where(
-            lane_col == 0,
-            mean_own,
-            jnp.where(
-                lane_col == 1,
-                jnp.sum(off * off, axis=1, keepdims=True),
-                jnp.where(
-                    lane_col == 2,
-                    jnp.sum(g, axis=1, keepdims=True),
-                    jnp.sum(g * off, axis=1, keepdims=True),
-                ),
-            ),
+        off = att - jnp.mean(att, axis=1, keepdims=True)
+        put_stats(
+            SG, at, jnp.sum(g, axis=1, keepdims=True), jnp.sum(g * off, axis=1, keepdims=True)
         )
-        ST[pid, :, at] = packed.T[:8]
-    st_peers = ((sib, z), (me, zp), (sib, zp))
-    st_slots = (2 * p + 1 - k, 2 * (1 - p) + k, 2 * (1 - p) + 1 - k)
-    st_sends = [
-        remote(ST.at[pid], ST.at[pid], stsend.at[i], strecv.at[pid], peer)
-        for i, peer in enumerate(st_peers)
-    ]
-    for copy in st_sends:
+    for copy in stat_sends(SG, sgsend, sgrecv):
         copy.start()
     for slot in st_slots:
-        arrived(ST.at[slot], strecv.at[slot])
-    means = [ST[q, 0:1, :] for q in range(4)]
+        arrived(SA.at[slot], sarecv.at[slot])
+    means = [SA[q, 0:1, :] for q in range(4)]
     mean = sum(means[1:], means[0]) / 4.0
     shifts = [m - mean for m in means]
-    squares = sum(ST[q, 1:2, :] + own_width * shifts[q] * shifts[q] for q in range(4))
+    squares = sum(SA[q, 1:2, :] + own_width * shifts[q] * shifts[q] for q in range(4))
     rstd = lax.rsqrt(squares / width + EPS)
-    g_mean = sum(ST[q, 2:3, :] for q in range(4)) / width
-    g_dot = rstd * sum(ST[q, 3:4, :] + shifts[q] * ST[q, 2:3, :] for q in range(4)) / width
-    table = jnp.concatenate([mean, rstd, g_mean, g_dot, mean, rstd, g_mean, g_dot], axis=0)
-    for b in range(n_seq):
-        at = slice(b * tok, (b + 1) * tok)
-        turned = jnp.concatenate([table[:, at]] * (DH // 8), axis=0).T
-        mean_c, rstd_c, g_mean_c, g_dot_c = [turned[:, q : q + 1] for q in range(4)]
-        d_mix, gate = DM[at, :], GT[at, :]
-        hat = (ATT[at, :] - mean_c) * rstd_c
-        normed_att = hat * gain
-        MR[at, :] = (normed_att * gate).astype(BF16)
-        DG[at, :] = d_mix * normed_att
-        DA[at, :] = (rstd_c * (d_mix * gate * gain - g_mean_c - hat * g_dot_c)).astype(BF16)
+    TB[...] = jnp.concatenate([mean, rstd] * 4, axis=0)
+
+    def turned(at):
+        return jnp.concatenate([TB[:, at]] * (DH // 8), axis=0).T
 
     def block_at(i):
         return (1 - ks) * (n_seq - 1 - i) + ks * i
@@ -586,8 +602,8 @@
                 CS[o, i] = pair_sum(o, i).astype(BF16)
                 cross_send(o, i).start()
 
-    def finish(o):
-        for i in range(n_seq):
+    def finish(o, which):
+        for i in which:
 
             @pl.when(jnp.logical_not(sends_cross(i)))
             def _():
@@ -606,10 +622,17 @@
                         home_send(o, i).start()
 
     for i in range(n_seq):
-        put_partial(0, i, mm(MR[rows_of(tok, block_at(i)), :], wo_heads, ((1,), (0,))))
+        at = rows_of(tok, block_at(i))
+        columns = turned(at)
+        hat = (ATT[at, :] - columns[:, 0:1]) * columns[:, 1:2]
+        ATT[at, :] = hat
+        mixed_rows = (hat * gain * GT[at, :]).astype(BF16)
+        MR[at, :] = mixed_rows
+        put_partial(0, i, mm(mixed_rows, wo_heads, ((1,), (0,))))
         if i > 0:
             pair_send(0, i - 1).start()
     pair_send(0, last).start()
+    cross(0)
 
     def g_send(j):
         return remote(MW.at[j], WG.at[chip], gsend.at[j], grecv.at[chip], (2 * (2 * k + j) + p, z))
@@ -619,7 +642,6 @@
 
     for j in range(2):
         MW[j] = mm(MR[:, j * DH : (j + 1) * DH], c_rows, ((0,), (0,))).astype(BF16)
-    cross(0)
     for j in range(2):
 
         @pl.when(g_self(j))
@@ -631,14 +653,16 @@
             g_send(j).start()
 
     is_root = k == p
-    centre = 2 - k
-    is_centre = z == centre
-
-    def h_send():
-        return remote(PS, PR, hsem.at[0], hsem.at[1], (me, lax.rem(z + 2, n_seq)))
-
-    def t_send(i):
-        return remote(TS, TR, tsend.at[i], trecv, (me, z - 1 + 2 * i))
+    far_root, near_root, middle, edge = (n_seq - 1) * k, 2 - k, 1 + k, (n_seq - 1) * (1 - k)
+
+    def h_send(dst, recv):
+        return remote(PS, dst, hsem.at[0], hsem.at[recv], (me, middle))
+
+    def h_relay(src, i, to):
+        return remote(src, PR, tsend.at[i], hsem.at[3], (me, to))
+
+    def t_send():
+        return remote(TS, TR, tsend.at[2], trecv, (me, edge))
 
     def plane_sum():
         @pl.when(is_root)
@@ -649,19 +673,44 @@
             for c in range(1, n_dp // 2):
                 total = total + WG[c].astype(F32)
             PS[...] = total.astype(BF16)
-            h_send().start()
-
-    def plane_total():
-        @pl.when(is_root)
-        def _():
-            arrived(PR, hsem.at[1])
-            TS[...] = (PS[...].astype(F32) + PR[...].astype(F32)).astype(BF16)
-            wg_ref[...] = TS[...].astype(F32)
-
-            @pl.when(is_centre)
+
+            @pl.when(z == far_root)
             def _():
-                for i in range(2):
-                    t_send(i).start()
+                h_send(MA, 1).start()
+
+            @pl.when(z == near_root)
+            def _():
+                h_send(MB, 2).start()
+
+    def pass_sums():
+        @pl.when(z == middle)
+        def _():
+            arrived(MB, hsem.at[2])
+            h_relay(MB, 0, far_root).start()
+            arrived(MA, hsem.at[1])
+            h_relay(MA, 1, near_root).start()
+            wg_ref[...] = (MA[...].astype(F32) + MB[...].astype(F32)).astype(BF16)
+
+    def root_total():
+        arrived(PR, hsem.at[3])
+        TS[...] = (PS[...].astype(F32) + PR[...].astype(F32)).astype(BF16)
+        wg_ref[...] = TS[...]
+
+    def near_total():
+        @pl.when(z == near_root)
+        def _():
+            root_total()
+            t_send().start()
+
+    def outer_total():
+        @pl.when(z == far_root)
+        def _():
+            root_total()
+
+        @pl.when(z == edge)
+        def _():
+            arrived(TR, trecv)
+            wg_ref[...] = TR[...]
 
     def backward(j):
         values, queries, keys = [ACT[j, g] for g in range(3)]
@@ -689,9 +738,22 @@
         put(1, 0, rows, VA[...])
         put(3, 0, rows, KA[...] * scale)
 
+    for slot in st_slots:
+        arrived(SG.at[slot], sgrecv.at[slot])
+    g_mean = sum(SG[q, 0:1, :] for q in range(4)) / width
+    g_dot = rstd * sum(SG[q, 1:2, :] + shifts[q] * SG[q, 0:1, :] for q in range(4)) / width
+    TB[...] = jnp.concatenate([rstd, g_mean, g_dot, rstd] * 2, axis=0)
+    for b in range(n_seq):
+        at = slice(b * tok, (b + 1) * tok)
+        columns = turned(at)
+        d_mix, hat = DM[at, :], ATT[at, :]
+        DG[at, :] = d_mix * (hat * gain)
+        g = d_mix * GT[at, :] * gain
+        DA[at, :] = (
+            columns[:, 0:1] * (g - columns[:, 1:2] - hat * columns[:, 2:3])
+        ).astype(BF16)
+
     backward(0)
-    finish(0)
-    plane_sum()
     backward(1)
     for i in range(n_seq):
         at = rows_of(tok, block_at(i))
@@ -700,25 +762,26 @@
         )
         if i > 0:
             pair_send(1, i - 1).start()
+            finish(0, (i - 1,))
     pair_send(1, last).start()
+    plane_sum()
     cross(1)
-    plane_total()
-    finish(1)
+    finish(0, (last,))
+    pass_sums()
+    finish(1, (0,))
+    near_total()
+    finish(1, (1, 2, 3))
 
     for h in range(2):
         arrived(RO.at[0, h], orecv.at[0, h])
     wide = x_ref[...].astype(F32)
     mixed_ref[...] = (wide + RO[0].reshape(tok, width).astype(F32)).astype(BF16)
 
-    @pl.when(jnp.logical_not(is_root))
-    def _():
-        arrived(TR, trecv)
-        wg_ref[...] = TR[...].astype(F32)
-
     average = jnp.mean(wide, axis=-1, keepdims=True)
     centred = wide - average
     inv = lax.rsqrt(jnp.mean(centred * centred, axis=-1, keepdims=True) + EPS)
     hat = centred * inv
+    outer_total()
     for h in range(2):
         arrived(RO.at[1, h], orecv.at[1, h])
     grad = RO[1].reshape(tok, width).astype(F32) * gin_ref[...]
@@ -768,17 +831,21 @@
         def _():
             wo_sends[3].wait_send()
 
-    for copy in st_sends:
+    for copy in stat_sends(SA, sasend, sarecv) + stat_sends(SG, sgsend, sgrecv):
         copy.wait_send()
 
     @pl.when(is_root)
     def _():
-        h_send().wait_send()
-
-        @pl.when(is_centre)
-        def _():
-            for i in range(2):
-                t_send(i).wait_send()
+        h_send(MA, 1).wait_send()
+
+    @pl.when(z == near_root)
+    def _():
+        t_send().wait_send()
+
+    @pl.when(z == middle)
+    def _():
+        h_relay(MB, 0, far_root).wait_send()
+        h_relay(MA, 1, near_root).wait_send()
 
     for o in range(2):
         for i in range(n_seq):
@@ -791,6 +858,21 @@
             @pl.when(jnp.logical_not(sends_cross(i)) & jnp.logical_not(home_is_self(i)))
             def _():
                 home_send(o, i).wait_send()
+
+
+def tail_kernel(mixed_ref, grad_ref, wg_ref, mixed_out, grad_out, wg_out, wide, sems):
+    copies = [
+        pltpu.make_async_copy(src, dst, sems.at[i])
+        for i, (src, dst) in enumerate(
+            ((mixed_ref, mixed_out), (grad_ref, grad_out), (wide, wg_out))
+        )
+    ]
+    copies[0].start()
+    copies[1].start()
+    wide[...] = wg_ref[...].astype(F32)
+    copies[2].start()
+    for copy in copies:
+        copy.wait()
 
 
 def column_parallel(
@@ -798,29 +880,40 @@
 ):
     tok, width = tokens.shape[1:]
     rows = tok * n_seq
-    meta = jnp.concatenate([stamps.reshape(-1, DH), jnp.broadcast_to(lengths[:, None], (4, DH))])
     dma = pltpu.SemaphoreType.DMA
     sds = jax.ShapeDtypeStruct
-    smem = pl.BlockSpec(memory_space=pltpu.SMEM)
+    hbm = pl.BlockSpec(memory_space=pltpu.HBM)
 
     def vb(*shape):
         return pltpu.VMEM(shape, BF16)
 
     def vf(*shape):
         return pltpu.VMEM(shape, F32)
+
+    def in_hbm(value):
+        return pltpu.with_memory_space_constraint(value, pltpu.HBM)
 
     half = tok // 2
     mixed, grad, w_grad = pl.pallas_call(
         lambda *refs: column_kernel(n_dp, n_seq, *refs),
-        out_shape=(sds((tok, width), BF16), sds((tok, width), BF16), sds(w_out.shape, F32)),
-        in_specs=[VM] * 7 + [smem],
+        out_shape=(sds((tok, width), BF16), sds((tok, width), BF16), sds(w_out.shape, BF16)),
+        in_specs=[hbm] * 5 + [pl.BlockSpec(memory_space=pltpu.SMEM)] + [hbm] * 3,
         out_specs=[VM] * 3,
         scratch_shapes=[
+            pltpu.VMEM(w_qkvu.shape, BF16),
+            vb(tok, width),
+            vb(tok, width),
+            vb(DH, width),
+            pltpu.VMEM(stamps.shape, jnp.int32),
+            vf(1, width),
+            vf(1, width),
+            pltpu.SMEM(bias_table.shape, F32),
+            pltpu.VMEM((8, rows), jnp.int32),
             vb(2, width, 4 * DH),
             vb(n_seq, tok, width),
             vb(n_seq, tok, width),
             vb(2, DH, width),
-            pltpu.VMEM(meta.shape, jnp.int32),
+            pltpu.VMEM((8, rows), jnp.int32),
             vb(rows, width),
             vf(2, rows, rows),
             vf(2, rows, 4 * DH),
@@ -837,8 +930,12 @@
             vf(rows, DH),
             vf(rows, DH),
             vf(4, 8, rows),
+            vf(4, 8, rows),
+            vf(8, rows),
             vb(2, DH, width),
             vb(n_dp // 2, DH, width),
+            vb(DH, width),
+            vb(DH, width),
             vb(DH, width),
             vb(DH, width),
             vb(DH, width),
@@ -849,6 +946,7 @@
             vb(2, n_seq, half, width),
             vb(2, n_seq, half, width),
             vb(2, 2, half, width),
+            dma((8,)),
             dma((5, 2)),
             dma((2, 2)),
             dma((n_dp, 2)),
@@ -861,10 +959,12 @@
             dma((2,)),
             dma((3,)),
             dma((4,)),
+            dma((3,)),
+            dma((4,)),
             dma((2,)),
             dma((n_dp // 2,)),
-            dma((2,)),
-            dma((2,)),
+            dma((4,)),
+            dma((3,)),
             dma,
             dma((2, n_seq)),
             dma((2, n_seq)),
@@ -873,11 +973,24 @@
             dma((2, n_seq)),
             dma((2, 2)),
         ],
-        compiler_params=pltpu.CompilerParams(has_side_effects=True),
+        compiler_params=pltpu.CompilerParams(
+            has_side_effects=True, collective_id=0, vmem_limit_bytes=44 * 2**20
+        ),
         name="column",
     )(
-        w_qkvu, tokens[0], cotangent[0], w_out, meta, gain_in[None], gain_out[None], bias_table
-    )
+        *[in_hbm(v) for v in (w_qkvu, tokens[0], cotangent[0], w_out, stamps)],
+        lengths,
+        *[in_hbm(v) for v in (gain_in[None], gain_out[None], bias_table)],
+    )
+    mixed, grad, w_grad = pl.pallas_call(
+        tail_kernel,
+        out_shape=(sds(mixed.shape, BF16), sds(grad.shape, BF16), sds(w_grad.shape, F32)),
+        in_specs=[VM] * 3,
+        out_specs=[hbm] * 3,
+        scratch_shapes=[vf(*w_grad.shape), dma((3,))],
+        compiler_params=pltpu.CompilerParams(vmem_limit_bytes=8 * 2**20),
+        name="tail",
+    )(mixed, grad, w_grad)
     return (mixed[None], grad[None], w_grad)
 
 

time: 75.6 us -> 63.1 us (0.83)
  Pallas kernels: 69.6 us -> 61.6 us
  local copies, waits for them, and re-layouts: 4.51 us -> 0 us
    pallas_call x1, Pallas kernels: 69.6 us -> 60.6 us  [column_parallel(): pl.pallas_call(lambda *refs: column_kernel(n_dp, n_seq, *refs), out_shape...]
    unnamed x9 -> x0, local copies, waits for them, and re-layouts: 3.92 us -> none
    pallas_call x0 -> x1, Pallas kernels: none -> 0.99 us  [column_parallel(): pl.pallas_call(tail_kernel, out_shape=(sds(mixed.shape, BF16), sds(grad.s...]
where the time goes in v2:
time: 63.1 us; the launch traced here: 62.9 us
  Pallas kernels  61.6 us (98%)
  between operations  1.29 us (2%)
    pallas_call x1, Pallas kernels, column_parallel(): pl.pallas_call(lambda *refs: column_kernel(n_dp, n_seq, *refs), out_shape...  60.6 us

profile of v2, /device:TPU:1, one launch (start us, length us, event | category | flops | bytes accessed | tf_op | source)
XLA Modules:
  0.0 62.9 jit_solution(3514502973939064598)
XLA Ops:
  1.3 60.6 %column.1 = (bf16[128,1024]{1,0:T(8,128)(2,1)S(1)}, bf16[128,1024]{1,0:T(8,128)(2,1)S(1)}, bf16[128,1024]{1,0:T(8,128)(2,1)S(1)}) custom-call(bf16[128,4096]{1,0:T(8,128)(2,1)} %refs_0_.1, bf16[128,1024]{1,0:T(8,128)(2,1)} %bitcast.6, bf16[128,1024]{1,0:T(8,128)(2,1)} %bitcast.7, bf16[128,1024]{1,0:T(8,128)(2,1)} %refs_3_.1, s32[1,512]{1,0:T(1,128)} %refs_4_.1, ...), custom_call_target="tpu_custom_call" | custom-call | tf_op jit(solution)/shard_map/column/pallas_call | solution.py:897
  61.9 1.0 %tail.1 = (bf16[128,1024]{1,0:T(8,128)(2,1)}, bf16[128,1024]{1,0:T(8,128)(2,1)}, f32[128,1024]{1,0:T(8,128)}) custom-call(bf16[128,1024]{1,0:T(8,128)(2,1)S(1)} %get-tuple-element.9.mixed_ref, bf16[128,1024]{1,0:T(8,128)(2,1)S(1)} %get-tuple-element.10.grad_ref, bf16[128,1024]{1,0:T(8,128)(2,1)S(1)} %get-tuple-element.11.wg_ref), custom_call_target="tpu_custom_call" | custom-call | tf_op jit(solution)/shard_map/tail/pallas_call | solution.py:985

commit v3 on v2

--- a/solution.py
+++ b/solution.py
@@ -229,6 +229,7 @@
 F32 = jnp.float32
 BF16 = jnp.bfloat16
 MASKED = -1e30
+PIECES = 4
 
 
 def mm(a, b, dims):
@@ -250,14 +251,19 @@
     pltpu.make_async_copy(dst, dst, sem).wait()
 
 
+def sent(block, sem, target):
+    remote(block, block, sem, sem, target).wait_send()
+
+
 def column_kernel(
     n_dp, n_seq, w_hbm, x_hbm, c_hbm, wo_hbm, stamps_hbm, length_ref, gin_hbm, gout_hbm, bias_hbm,
     mixed_ref, grad_ref, wg_ref,
     w_ref, x_ref, c_ref, wo_ref, stamps_ref, gin_ref, gout_ref, bias_ref, meta_ref,
-    W, X, C, WO, mbuf, NB, BI, PJ, GT, ACT, ATT, WT, SL, DM, DG, DA, DP, MR, KA, VA, SA, SG, TB,
+    W, X, C, WO, mbuf, NB, BI, PJ, GT, ACT, ATT, WT, SL, DM, DG, DA, DP, MR, MX, KA, VA, SA, SG, TB,
     MW, WG, PS, PR, TS, TR, MA, MB, PB, SB, CS, FB, FIN, RO,
-    lsem, wsend, wrelay, wrecv, zsend, ssend, farsend, xrecv, wosend, worecv, msem,
-    sasend, sarecv, sgsend, sgrecv, gsend, grecv, hsem, tsend, trecv, psend, precv, csend, crecv, osend, orecv,
+    lsem, wout, wvia, wrest, zout, shareout, farout, xrecv, woout, worecv, msem,
+    saout, sarecv, sgout, sgrecv, mxout, mxrecv, gout, grecv,
+    hout, hmid, hback, trecv, pout, precv, cout, crecv, oout, orecv,
 ):
     me = lax.axis_index("dp")
     z = lax.axis_index("seq")
@@ -297,13 +303,15 @@
             for g in range(4)
         ]
 
-    w_targets = ((xn, 0, 1), (yn, 1, 4), (chip, 1 - k, 0), (xn, 1, 2), (yn, 0, 3))
+    w_targets = (
+        (xn, 0, wvia.at[k]), (yn, 1, wvia.at[k]), (chip, 1 - k, wrest), (xn, 1, wrest),
+        (yn, 0, wrest),
+    )
 
     def w_start(j):
-        for where, core, index in w_targets:
+        for where, core, sem in w_targets:
             for copy in w_copies(
-                core, j,
-                lambda s, d: remote(s, d, wsend.at[index, j], wrecv.at[me, j], (2 * where + core, z)),
+                core, j, lambda s, d: remote(s, d, wout, sem.at[j], (2 * where + core, z))
             ):
                 copy.start()
 
@@ -315,16 +323,13 @@
     def w_relay(i, j):
         src = 2 * via + i
         block = w_piece(src, j)
-        return remote(block, block, wrelay.at[i, j], wrecv.at[src, j], (2 * to + k, z))
-
-    def w_wait(src, j):
-        arrived(w_piece(src, j), wrecv.at[src, j])
+        return remote(block, block, wout, wrest.at[j], (2 * to + k, z))
 
     ins, outs = (x_ref, c_ref), (X, C)
     z_to = jnp.where(is_main, zp, 1 + k)
 
     def z_send(a):
-        return remote(ins[a], outs[a].at[z], zsend.at[a], xrecv.at[a, z], (me, z_to))
+        return remote(ins[a], outs[a].at[z], zout, xrecv.at[a, z], (me, z_to))
 
     def own_copy(a):
         return pltpu.make_async_copy(ins[a], outs[a].at[z], xrecv.at[a, z])
@@ -332,13 +337,13 @@
     def share(a, b):
         block = ins[a] if b is None else outs[a].at[b]
         at = z if b is None else b
-        return remote(block, outs[a].at[at], ssend.at[a, at], xrecv.at[a, at], (sib, z))
+        return remote(block, outs[a].at[at], shareout, xrecv.at[a, at], (sib, z))
 
     foreign = (2 * (1 - ks), 2 * (1 - ks) + 1)
 
     def to_far(a, i):
         block = outs[a].at[foreign[i]]
-        return remote(block, block, farsend.at[a, i], xrecv.at[a, foreign[i]], (me, far))
+        return remote(block, block, farout, xrecv.at[a, foreign[i]], (me, far))
 
     def x_wait(a, b):
         arrived(outs[a].at[b], xrecv.at[a, b])
@@ -347,19 +352,39 @@
         return remote(meta_ref, mbuf, msem.at[0], msem.at[1], (sib, z))
 
     wo_core, wo_slot = chip // 2, chip % 2
+    wo_part = 2 * k + wo_core
     wo_here = wo_core == k
+    wo_sem = jnp.where(k == p, wo_slot, 2)
     wo_sends = [
-        remote(wo_ref, WO.at[wo_slot], wosend.at[i], worecv.at[wo_slot], (2 * where + wo_core, z))
+        remote(
+            wo_ref, WO.at[wo_part, wo_slot], woout, worecv.at[wo_sem],
+            (2 * where + wo_core, z),
+        )
         for i, where in enumerate((xn, yn, dn, chip))
     ]
 
+    def wo_start():
+        for i in range(3):
+            wo_sends[i].start()
+
+        @pl.when(wo_here)
+        def _():
+            pltpu.make_async_copy(wo_ref, WO.at[wo_part, wo_slot], worecv.at[wo_sem]).start()
+
+        @pl.when(jnp.logical_not(wo_here))
+        def _():
+            wo_sends[3].start()
+
+    def wo_share(parity, j):
+        block = WO.at[2 * parity + k, j]
+        return remote(block, block, woout, worecv.at[3], (sib, z))
+
     loads = [
         pltpu.make_async_copy(src, dst, lsem.at[i])
-        for i, (src, dst) in enumerate(
-            (
-                (stamps_hbm, stamps_ref), (w_hbm, w_ref), (x_hbm, x_ref), (c_hbm, c_ref),
-                (wo_hbm, wo_ref), (gin_hbm, gin_ref), (gout_hbm, gout_ref), (bias_hbm, bias_ref),
-            )
+        for src, dst, i in (
+            (stamps_hbm, stamps_ref, 0), (w_hbm, w_ref, 1), (x_hbm, x_ref, 1), (c_hbm, c_ref, 1),
+            (wo_hbm, wo_ref, 1), (gin_hbm, gin_ref, 2), (gout_hbm, gout_ref, 3),
+            (bias_hbm, bias_ref, 4),
         )
     ]
     barrier = pltpu.get_barrier_semaphore()
@@ -373,7 +398,8 @@
     loads[0].wait()
     meta_ref[0:1, :] = stamps_ref[...]
     meta_ref[1:2, :] = jnp.full(stamps_ref.shape, length_ref[0], jnp.int32)
-    for load in loads[1:]:
+    arrived(W.at[:, : (n_dp - 1) * tok], lsem.at[1])
+    for load in loads[5:]:
         load.wait()
     pl.semaphore_wait(barrier, len(peers))
     @pl.when(is_main)
@@ -397,12 +423,12 @@
         share(1, None).start()
 
     for j in range(2):
-        for copy in w_copies(k, j, lambda s, d: pltpu.make_async_copy(s, d, wrecv.at[me, j])):
+        for copy in w_copies(k, j, lambda s, d: pltpu.make_async_copy(s, d, wrest.at[j])):
             copy.start()
 
     def relay_weights(j):
         for i in range(2):
-            w_wait(2 * via + i, j)
+            arrived(w_piece(2 * via + i, j), wvia.at[i, j])
             w_relay(i, j).start()
 
     def near_relay(a):
@@ -454,19 +480,6 @@
     near_relay(1)
     relay_weights(1)
 
-    @pl.when(k == p)
-    def _():
-        for i in range(3):
-            wo_sends[i].start()
-
-        @pl.when(wo_here)
-        def _():
-            pltpu.make_async_copy(wo_ref, WO.at[wo_slot], worecv.at[wo_slot]).start()
-
-        @pl.when(jnp.logical_not(wo_here))
-        def _():
-            wo_sends[3].start()
-
     far_relay(0)
 
     @pl.when(is_main)
@@ -482,11 +495,7 @@
         NB[b * tok : (b + 1) * tok, :] = layer_norm(X[b].astype(F32), gin_ref[...]).astype(BF16)
 
     def forward(j):
-        w_wait(me, j)
-        w_wait(sib, j)
-        for i in range(2):
-            w_wait(2 * to + i, j)
-            w_wait(2 * dn + i, j)
+        arrived(W.at[j, : (n_dp - 2) * tok], wrest.at[j])
         PJ[j] = mm(NB[...], W[j], ((1,), (0,)))
         cols = slice(j * DH, (j + 1) * DH)
         GT[:, cols] = jax.nn.silu(PJ[j, :, :DH])
@@ -501,19 +510,23 @@
             SL[j, at, :end] = sig * (1.0 + scores * (1.0 - sig))
             ATT[at, cols] = mm(weight, ACT[j, 0, :end], ((1,), (0,)))
 
+    @pl.when(k == p)
+    def _():
+        wo_start()
+
     forward(0)
+
     forward(1)
 
     gain = jnp.concatenate([gout_ref[:, lanes_of(head_of(k, j))] for j in range(2)], axis=1)
     pid = 2 * p + k
     own_width = 2 * DH
     st_peers = ((sib, z), (me, zp), (sib, zp))
-    st_slots = (2 * p + 1 - k, 2 * (1 - p) + k, 2 * (1 - p) + 1 - k)
 
     def stat_sends(ref, send_sem, recv_sem):
         return [
-            remote(ref.at[pid], ref.at[pid], send_sem.at[i], recv_sem.at[pid], peer)
-            for i, peer in enumerate(st_peers)
+            remote(ref.at[pid], ref.at[pid], send_sem, recv_sem, peer)
+            for peer in st_peers
         ]
 
     def put_stats(ref, at, first, second):
@@ -525,12 +538,9 @@
         mean_own = jnp.mean(att, axis=1, keepdims=True)
         off = att - mean_own
         put_stats(SA, at, mean_own, jnp.sum(off * off, axis=1, keepdims=True))
-    for copy in stat_sends(SA, sasend, sarecv):
+    for copy in stat_sends(SA, saout, sarecv):
         copy.start()
     far_relay(1)
-    for j in range(2):
-        arrived(WO.at[j], worecv.at[j])
-    wo_heads = WO[...].reshape(2 * DH, width)
     @pl.when(is_main)
     def _():
         x_wait(1, z)
@@ -541,19 +551,22 @@
             x_wait(1, b)
 
     c_rows = C[...].reshape(rows, width)
-    DM[...] = mm(c_rows, wo_heads, ((1,), (1,)))
+    for j in range(2):
+        arrived(WO.at[pid, j], worecv.at[j])
+        wo_share(p, j).start()
+        DM[:, j * DH : (j + 1) * DH] = mm(c_rows, WO[pid, j], ((1,), (1,)))
     for b in range(n_seq):
         at = slice(b * tok, (b + 1) * tok)
         att = ATT[at, :]
+        off = att - jnp.mean(att, axis=1, keepdims=True)
         g = DM[at, :] * GT[at, :] * gain
-        off = att - jnp.mean(att, axis=1, keepdims=True)
         put_stats(
             SG, at, jnp.sum(g, axis=1, keepdims=True), jnp.sum(g * off, axis=1, keepdims=True)
         )
-    for copy in stat_sends(SG, sgsend, sgrecv):
+    for copy in stat_sends(SG, sgout, sgrecv):
         copy.start()
-    for slot in st_slots:
-        arrived(SA.at[slot], sarecv.at[slot])
+
+    arrived(SA.at[:3], sarecv)
     means = [SA[q, 0:1, :] for q in range(4)]
     mean = sum(means[1:], means[0]) / 4.0
     shifts = [m - mean for m in means]
@@ -564,182 +577,173 @@
     def turned(at):
         return jnp.concatenate([TB[:, at]] * (DH // 8), axis=0).T
 
-    def block_at(i):
-        return (1 - ks) * (n_seq - 1 - i) + ks * i
-
-    def pair_send(o, i):
-        return remote(PB.at[o, i, 1 - k], SB.at[o, i], psend.at[o, i], precv.at[o, i], (sib, z))
-
-    def cross_send(o, i):
-        return remote(CS.at[o, i], FB.at[o, i], csend.at[o, i], crecv.at[o, i], (me, zp))
-
-    def home_is_self(i):
-        return is_main & (block_at(i) == z)
-
-    def home_send(o, i):
+    blocks = tuple(reversed(range(n_seq)))
+
+    def mine(b):
+        return is_near == (far != b)
+
+    def other(b):
+        return is_near == (far == b)
+
+    def home_is_self(b):
+        return is_main & (z == b)
+
+    def mx_send(b):
         return remote(
-            FIN.at[o, i], RO.at[o, k], osend.at[o, i], orecv.at[o, k], (main_dp, block_at(i))
+            MR.at[b * tok : (b + 1) * tok], MX.at[pid], mxout, mxrecv, (main_dp, b)
         )
 
-    last = n_seq - 1
-
-    def sends_cross(i):
-        return is_near if i == last else is_far
-
-    def put_partial(o, i, part):
-        PB[o, i, 0] = part[:half].astype(BF16)
-        PB[o, i, 1] = part[half:].astype(BF16)
-
-    def pair_sum(o, i):
-        return PB[o, i, k].astype(F32) + SB[o, i].astype(F32)
-
-    def cross(o):
-        for i in range(n_seq):
-            arrived(SB.at[o, i], precv.at[o, i])
-
-            @pl.when(sends_cross(i))
-            def _():
-                CS[o, i] = pair_sum(o, i).astype(BF16)
-                cross_send(o, i).start()
-
-    def finish(o, which):
-        for i in which:
-
-            @pl.when(jnp.logical_not(sends_cross(i)))
-            def _():
-                arrived(FB.at[o, i], crecv.at[o, i])
-                FIN[o, i] = (pair_sum(o, i) + FB[o, i].astype(F32)).astype(BF16)
-                if i < 2:
-                    home_send(o, i).start()
-                else:
-
-                    @pl.when(home_is_self(i))
-                    def _():
-                        pltpu.make_async_copy(FIN.at[o, i], RO.at[o, k], orecv.at[o, k]).start()
-
-                    @pl.when(jnp.logical_not(home_is_self(i)))
-                    def _():
-                        home_send(o, i).start()
-
-    for i in range(n_seq):
-        at = rows_of(tok, block_at(i))
+    for b in blocks:
+        at = slice(b * tok, (b + 1) * tok)
         columns = turned(at)
         hat = (ATT[at, :] - columns[:, 0:1]) * columns[:, 1:2]
         ATT[at, :] = hat
-        mixed_rows = (hat * gain * GT[at, :]).astype(BF16)
-        MR[at, :] = mixed_rows
-        put_partial(0, i, mm(mixed_rows, wo_heads, ((1,), (0,))))
-        if i > 0:
-            pair_send(0, i - 1).start()
-    pair_send(0, last).start()
-    cross(0)
-
-    def g_send(j):
-        return remote(MW.at[j], WG.at[chip], gsend.at[j], grecv.at[chip], (2 * (2 * k + j) + p, z))
+        MR[at, :] = (hat * gain * GT[at, :]).astype(BF16)
+
+    for b in blocks:
+
+        @pl.when(home_is_self(b))
+        def _():
+            pltpu.make_async_copy(
+                MR.at[b * tok : (b + 1) * tok], MX.at[pid], mxrecv
+            ).start()
+
+        @pl.when(jnp.logical_not(home_is_self(b)))
+        def _():
+            mx_send(b).start()
+
+    pieces = PIECES
+    piece = DH // pieces
+
+    def out_rows(i):
+        return slice(i * piece, (i + 1) * piece)
+
+    def g_send(j, i):
+        return remote(
+            MW.at[j, i], WG.at[chip, i], gout, grecv.at[i],
+            (2 * (2 * k + j) + p, z),
+        )
 
     def g_self(j):
         return (2 * k + j == chip) & (k == p)
 
     for j in range(2):
-        MW[j] = mm(MR[:, j * DH : (j + 1) * DH], c_rows, ((0,), (0,))).astype(BF16)
-    for j in range(2):
-
-        @pl.when(g_self(j))
-        def _():
-            pltpu.make_async_copy(MW.at[j], WG.at[chip], grecv.at[chip]).start()
-
-        @pl.when(jnp.logical_not(g_self(j)))
-        def _():
-            g_send(j).start()
+        part = mm(MR[:, j * DH : (j + 1) * DH], c_rows, ((0,), (0,)))
+        for i in range(pieces):
+            MW[j, i] = part[out_rows(i)].astype(BF16)
+    for i in range(pieces):
+        for j in range(2):
+
+            @pl.when(g_self(j))
+            def _():
+                pltpu.make_async_copy(MW.at[j, i], WG.at[chip, i], grecv.at[i]).start()
+
+            @pl.when(jnp.logical_not(g_self(j)))
+            def _():
+                g_send(j, i).start()
 
     is_root = k == p
     far_root, near_root, middle, edge = (n_seq - 1) * k, 2 - k, 1 + k, (n_seq - 1) * (1 - k)
-
-    def h_send(dst, recv):
-        return remote(PS, dst, hsem.at[0], hsem.at[recv], (me, middle))
+    def h_send(dst, recv, i):
+        return remote(PS.at[i], dst.at[i], hout, recv.at[i], (me, middle))
 
     def h_relay(src, i, to):
-        return remote(src, PR, tsend.at[i], hsem.at[3], (me, to))
-
-    def t_send():
-        return remote(TS, TR, tsend.at[2], trecv, (me, edge))
-
-    def plane_sum():
+        return remote(src.at[i], PR.at[i], hout, hback.at[i], (me, to))
+
+    def t_send(i):
+        return remote(TS.at[i], TR.at[i], hout, trecv.at[i], (me, edge))
+
+    def plane_sum(i):
         @pl.when(is_root)
         def _():
-            for c in range(n_dp // 2):
-                arrived(WG.at[c], grecv.at[c])
-            total = WG[0].astype(F32)
+            arrived(WG.at[:, i], grecv.at[i])
+            total = WG[0, i].astype(F32)
             for c in range(1, n_dp // 2):
-                total = total + WG[c].astype(F32)
-            PS[...] = total.astype(BF16)
+                total = total + WG[c, i].astype(F32)
+            PS[i] = total.astype(BF16)
 
             @pl.when(z == far_root)
             def _():
-                h_send(MA, 1).start()
+                h_send(MA, hmid.at[0], i).start()
 
             @pl.when(z == near_root)
             def _():
-                h_send(MB, 2).start()
-
-    def pass_sums():
+                h_send(MB, hmid.at[1], i).start()
+
+    def pass_in():
         @pl.when(z == middle)
         def _():
-            arrived(MB, hsem.at[2])
-            h_relay(MB, 0, far_root).start()
-            arrived(MA, hsem.at[1])
-            h_relay(MA, 1, near_root).start()
-            wg_ref[...] = (MA[...].astype(F32) + MB[...].astype(F32)).astype(BF16)
-
-    def root_total():
-        arrived(PR, hsem.at[3])
-        TS[...] = (PS[...].astype(F32) + PR[...].astype(F32)).astype(BF16)
-        wg_ref[...] = TS[...]
+            for i in range(pieces):
+                arrived(MB.at[i], hmid.at[1, i])
+                h_relay(MB, i, far_root).start()
+
+    def pass_out():
+        @pl.when(z == middle)
+        def _():
+            for i in range(pieces):
+                arrived(MA.at[i], hmid.at[0, i])
+                h_relay(MA, i, near_root).start()
+                wg_ref[out_rows(i)] = (MA[i].astype(F32) + MB[i].astype(F32)).astype(BF16)
+
+    def root_total(i):
+        arrived(PR.at[i], hback.at[i])
+        TS[i] = (PS[i].astype(F32) + PR[i].astype(F32)).astype(BF16)
+        wg_ref[out_rows(i)] = TS[i]
 
     def near_total():
         @pl.when(z == near_root)
         def _():
-            root_total()
-            t_send().start()
+            for i in range(pieces):
+                root_total(i)
+                t_send(i).start()
 
     def outer_total():
         @pl.when(z == far_root)
         def _():
-            root_total()
+            for i in range(pieces):
+                root_total(i)
 
         @pl.when(z == edge)
         def _():
-            arrived(TR, trecv)
-            wg_ref[...] = TR[...]
-
-    def backward(j):
-        values, queries, keys = [ACT[j, g] for g in range(3)]
-        cols = slice(j * DH, (j + 1) * DH)
-
-        def put(group, start, end, grad):
-            at = slice(group * DH, (group + 1) * DH)
-            DP[j, start:end, at] = (grad * silu_slope(PJ[j, start:end, at])).astype(BF16)
-
-        for i in reversed(range(n_seq)):
-            start, end = i * tok, (i + 1) * tok
-            d_att = DA[start:end, cols]
-            d_weight = mm(d_att, values[:end], ((1,), (1,)))
-            d_scores = (d_weight * SL[j, start:end, :end]).astype(BF16)
-            put(2, start, end, mm(d_scores, keys[:end], ((1,), (0,))) * scale)
-            k_part = mm(d_scores, queries[start:end], ((0,), (0,)))
-            v_part = mm(WT[j, start:end, :end], d_att, ((0,), (0,)))
-            if end == rows:
-                KA[...] = k_part
-                VA[...] = v_part
-            else:
-                KA[:end] += k_part
-                VA[:end] += v_part
-        put(0, 0, rows, DG[:, cols])
-        put(1, 0, rows, VA[...])
-        put(3, 0, rows, KA[...] * scale)
-
-    for slot in st_slots:
-        arrived(SG.at[slot], sgrecv.at[slot])
+            for i in range(pieces):
+                arrived(TR.at[i], trecv.at[i])
+                wg_ref[out_rows(i)] = TR[i]
+
+    def pair_send(b):
+        return remote(PB.at[b, 1 - k], SB.at[b], pout, precv.at[b], (sib, z))
+
+    def cross_send(b):
+        return remote(CS.at[b], FB.at[b], cout, crecv.at[b], (me, zp))
+
+    def home_send(b):
+        return remote(FIN.at[b], RO.at[k], oout, orecv, (main_dp, b))
+
+    def pair_sum(b):
+        return PB[b, k].astype(F32) + SB[b].astype(F32)
+
+    def cross(b):
+        arrived(SB.at[b], precv.at[b])
+
+        @pl.when(other(b))
+        def _():
+            CS[b] = pair_sum(b).astype(BF16)
+            cross_send(b).start()
+
+    def finish(b):
+        @pl.when(mine(b))
+        def _():
+            arrived(FB.at[b], crecv.at[b])
+            FIN[b] = (pair_sum(b) + FB[b].astype(F32)).astype(BF16)
+
+            @pl.when(home_is_self(b))
+            def _():
+                pltpu.make_async_copy(FIN.at[b], RO.at[k], orecv).start()
+
+            @pl.when(jnp.logical_not(home_is_self(b)))
+            def _():
+                home_send(b).start()
+
+    arrived(SG.at[:3], sgrecv)
     g_mean = sum(SG[q, 0:1, :] for q in range(4)) / width
     g_dot = rstd * sum(SG[q, 1:2, :] + shifts[q] * SG[q, 0:1, :] for q in range(4)) / width
     TB[...] = jnp.concatenate([rstd, g_mean, g_dot, rstd] * 2, axis=0)
@@ -753,38 +757,98 @@
             columns[:, 0:1] * (g - columns[:, 1:2] - hat * columns[:, 2:3])
         ).astype(BF16)
 
-    backward(0)
-    backward(1)
-    for i in range(n_seq):
-        at = rows_of(tok, block_at(i))
-        put_partial(
-            1, i, mm(DP[0, at, :], W[0], ((1,), (1,))) + mm(DP[1, at, :], W[1], ((1,), (1,)))
-        )
-        if i > 0:
-            pair_send(1, i - 1).start()
-            finish(0, (i - 1,))
-    pair_send(1, last).start()
-    plane_sum()
+    def backward(j, b):
+        cols = slice(j * DH, (j + 1) * DH)
+        start, end = b * tok, (b + 1) * tok
+
+        def put(group, grad):
+            at = slice(group * DH, (group + 1) * DH)
+            DP[j, start:end, at] = (grad * silu_slope(PJ[j, start:end, at])).astype(BF16)
+
+        d_att = DA[start:end, cols]
+        d_weight = mm(d_att, ACT[j, 0, :end], ((1,), (1,)))
+        d_scores = (d_weight * SL[j, start:end, :end]).astype(BF16)
+        put(2, mm(d_scores, ACT[j, 2, :end], ((1,), (0,))) * scale)
+        k_part = mm(d_scores, ACT[j, 1, start:end], ((0,), (0,)))
+        v_part = mm(WT[j, start:end, :end], d_att, ((0,), (0,)))
+        if end == rows:
+            KA[j] = k_part
+            VA[j] = v_part
+        else:
+            KA[j, :end] += k_part
+            VA[j, :end] += v_part
+        put(0, DG[start:end, cols])
+        put(1, VA[j, start:end])
+        put(3, KA[j, start:end] * scale)
+
+    def d_part(b):
+        at = slice(b * tok, (b + 1) * tok)
+        part = mm(DP[0, at], W[0], ((1,), (1,))) + mm(DP[1, at], W[1], ((1,), (1,)))
+        PB[b, 0] = part[:half].astype(BF16)
+        PB[b, 1] = part[half:].astype(BF16)
+        pair_send(b).start()
+
+    last = n_seq - 1
+    for b in blocks:
+        for j in range(2):
+            backward(j, b)
+        if b == last:
+
+            @pl.when(ks == 0)
+            def _():
+                d_part(last)
+
+        else:
+            d_part(b)
+        if b == last - 1:
+
+            @pl.when(ks == 0)
+            def _():
+                cross(last)
+
+        elif b == 1:
+            cross(2)
+        if b < 2:
+            for i in range(pieces // 2):
+                plane_sum((1 - b) * pieces // 2 + i)
     cross(1)
-    finish(0, (last,))
-    pass_sums()
-    finish(1, (0,))
+    cross(0)
+
+    @pl.when(k != p)
+    def _():
+        wo_start()
+
+    @pl.when(ks != 0)
+    def _():
+        d_part(last)
+        cross(last)
+
+    finish(3)
+    pass_in()
+    finish(2)
+    pass_out()
+    finish(1)
+    finish(0)
     near_total()
-    finish(1, (1, 2, 3))
-
-    for h in range(2):
-        arrived(RO.at[0, h], orecv.at[0, h])
+    arrived(WO.at[2 * (1 - p) + k], worecv.at[2])
+    for j in range(2):
+        wo_share(1 - p, j).start()
+
+    arrived(X, worecv.at[3])
+    arrived(MX, mxrecv)
     wide = x_ref[...].astype(F32)
-    mixed_ref[...] = (wide + RO[0].reshape(tok, width).astype(F32)).astype(BF16)
+    total = wide
+    for q in range(4):
+        total = total + mm(MX[q], WO[q].reshape(2 * DH, width), ((1,), (0,)))
+    mixed_ref[...] = total.astype(BF16)
 
     average = jnp.mean(wide, axis=-1, keepdims=True)
     centred = wide - average
     inv = lax.rsqrt(jnp.mean(centred * centred, axis=-1, keepdims=True) + EPS)
     hat = centred * inv
     outer_total()
-    for h in range(2):
-        arrived(RO.at[1, h], orecv.at[1, h])
-    grad = RO[1].reshape(tok, width).astype(F32) * gin_ref[...]
+    arrived(RO, orecv)
+    grad = RO[...].reshape(tok, width).astype(F32) * gin_ref[...]
     back = inv * (
         grad
         - jnp.mean(grad, axis=-1, keepdims=True)
@@ -792,72 +856,36 @@
     )
     grad_ref[...] = (c_ref[...].astype(F32) + back).astype(BF16)
 
-    for j in range(2):
-        for index in range(5):
-            block = w_piece(me, j)
-            remote(block, block, wsend.at[index, j], wrecv.at[me, j], (sib, z)).wait_send()
-        for i in range(2):
-            w_relay(i, j).wait_send()
-
-        @pl.when(jnp.logical_not(g_self(j)))
-        def _():
-            g_send(j).wait_send()
-
-    for a in range(2):
-        z_send(a).wait_send()
-
-        @pl.when(is_main)
-        def _():
-            share(a, None).wait_send()
-            share(a, zp).wait_send()
-            for i in range(2):
-                share(a, foreign[i]).wait_send()
-
-        @pl.when(is_main & is_near)
-        def _():
-            for i in range(2):
-                to_far(a, i).wait_send()
-
-    @pl.when(is_main)
-    def _():
-        meta_send().wait_send()
-
-    @pl.when(k == p)
-    def _():
-        for i in range(3):
-            wo_sends[i].wait_send()
-
-        @pl.when(jnp.logical_not(wo_here))
-        def _():
-            wo_sends[3].wait_send()
-
-    for copy in stat_sends(SA, sasend, sarecv) + stat_sends(SG, sgsend, sgrecv):
-        copy.wait_send()
-
-    @pl.when(is_root)
-    def _():
-        h_send(MA, 1).wait_send()
-
-    @pl.when(z == near_root)
-    def _():
-        t_send().wait_send()
-
-    @pl.when(z == middle)
-    def _():
-        h_relay(MB, 0, far_root).wait_send()
-        h_relay(MA, 1, near_root).wait_send()
-
-    for o in range(2):
-        for i in range(n_seq):
-            pair_send(o, i).wait_send()
-
-            @pl.when(sends_cross(i))
-            def _():
-                cross_send(o, i).wait_send()
-
-            @pl.when(jnp.logical_not(sends_cross(i)) & jnp.logical_not(home_is_self(i)))
-            def _():
-                home_send(o, i).wait_send()
+    beside = (sib, z)
+
+    def sent_when(condition, block, sem):
+        @pl.when(condition)
+        def _():
+            sent(block, sem, beside)
+
+    part = (n_dp - 1) * tok
+    sent(W.at[:, :part], wout, beside)
+    sent(X.at[:2], zout, beside)
+    sent_when(is_main, W, shareout)
+    sent_when(is_main & is_near, X, farout)
+    sent_when(is_main, meta_ref, msem.at[0])
+    sent_when(wo_here, W.at[:, :part], woout)
+    sent_when(jnp.logical_not(wo_here), W, woout)
+    sent(SA.at[:3], saout, beside)
+    sent(SG.at[:3], sgout, beside)
+    sent_when(is_main, MX.at[:3], mxout)
+    sent_when(is_aux, MX, mxout)
+    keeps_one = is_root & wo_here
+    sent_when(keeps_one, X.at[0], gout)
+    sent_when(jnp.logical_not(keeps_one), X.at[:2], gout)
+    sent_when(z == far_root, PS, hout)
+    sent_when((z == near_root) | (z == middle), X.at[:2], hout)
+    sent(X.at[:2], pout, beside)
+    sent_when(is_far, CS.at[:3], cout)
+    sent_when(is_near, CS.at[:1], cout)
+    sent_when(is_near & is_main, FIN.at[:2], oout)
+    sent_when(is_near & is_aux, FIN.at[:3], oout)
+    sent_when(is_far & is_aux, FIN.at[:1], oout)
 
 
 def tail_kernel(mixed_ref, grad_ref, wg_ref, mixed_out, grad_out, wg_out, wide, sems):
@@ -912,7 +940,7 @@
             vb(2, width, 4 * DH),
             vb(n_seq, tok, width),
             vb(n_seq, tok, width),
-            vb(2, DH, width),
+            vb(4, 2, DH, width),
             pltpu.VMEM((8, rows), jnp.int32),
             vb(rows, width),
             vf(2, rows, rows),
@@ -927,51 +955,55 @@
             vb(rows, 2 * DH),
             vb(2, rows, 4 * DH),
             vb(rows, 2 * DH),
-            vf(rows, DH),
-            vf(rows, DH),
+            vb(4, tok, 2 * DH),
+            vf(2, rows, DH),
+            vf(2, rows, DH),
             vf(4, 8, rows),
             vf(4, 8, rows),
             vf(8, rows),
-            vb(2, DH, width),
-            vb(n_dp // 2, DH, width),
-            vb(DH, width),
-            vb(DH, width),
-            vb(DH, width),
-            vb(DH, width),
-            vb(DH, width),
-            vb(DH, width),
-            vb(2, n_seq, 2, half, width),
-            vb(2, n_seq, half, width),
-            vb(2, n_seq, half, width),
-            vb(2, n_seq, half, width),
-            vb(2, n_seq, half, width),
-            vb(2, 2, half, width),
-            dma((8,)),
-            dma((5, 2)),
+            vb(2, PIECES, DH // PIECES, width),
+            vb(n_dp // 2, PIECES, DH // PIECES, width),
+            vb(PIECES, DH // PIECES, width),
+            vb(PIECES, DH // PIECES, width),
+            vb(PIECES, DH // PIECES, width),
+            vb(PIECES, DH // PIECES, width),
+            vb(PIECES, DH // PIECES, width),
+            vb(PIECES, DH // PIECES, width),
+            vb(n_seq, 2, half, width),
+            vb(n_seq, half, width),
+            vb(n_seq, half, width),
+            vb(n_seq, half, width),
+            vb(n_seq, half, width),
+            vb(2, half, width),
+            dma((5,)),
+            dma,
             dma((2, 2)),
-            dma((n_dp, 2)),
             dma((2,)),
+            dma,
+            dma,
+            dma,
             dma((2, n_seq)),
-            dma((2, 2)),
-            dma((2, n_seq)),
+            dma,
             dma((4,)),
             dma((2,)),
-            dma((2,)),
-            dma((3,)),
-            dma((4,)),
-            dma((3,)),
-            dma((4,)),
-            dma((2,)),
-            dma((n_dp // 2,)),
-            dma((4,)),
-            dma((3,)),
-            dma,
-            dma((2, n_seq)),
-            dma((2, n_seq)),
-            dma((2, n_seq)),
-            dma((2, n_seq)),
-            dma((2, n_seq)),
-            dma((2, 2)),
+            dma,
+            dma,
+            dma,
+            dma,
+            dma,
+            dma,
+            dma,
+            dma((PIECES,)),
+            dma,
+            dma((2, PIECES)),
+            dma((PIECES,)),
+            dma((PIECES,)),
+            dma,
+            dma((n_seq,)),
+            dma,
+            dma((n_seq,)),
+            dma,
+            dma,
         ],
         compiler_params=pltpu.CompilerParams(
             has_side_effects=True, collective_id=0, vmem_limit_bytes=44 * 2**20

time: 63.1 us -> 59.1 us (0.937)
  Pallas kernels: 61.6 us -> 57.6 us
    pallas_call x1, Pallas kernels: 60.6 us -> 56.6 us  [column_parallel(): pl.pallas_call(lambda *refs: column_kernel(n_dp, n_seq, *refs), out_shape...]
where the time goes in v3:
time: 59.1 us; the launch traced here: 58.9 us
  Pallas kernels  57.6 us (97%)
  between operations  1.29 us (2%)
    pallas_call x1, Pallas kernels, column_parallel(): pl.pallas_call(lambda *refs: column_kernel(n_dp, n_seq, *refs), out_shape...  56.6 us

profile of v3, /device:TPU:1, one launch (start us, length us, event | category | flops | bytes accessed | tf_op | source)
XLA Modules:
  0.0 58.9 jit_solution(15302238208165484485)
XLA Ops:
  1.3 56.6 %column.1 = (bf16[128,1024]{1,0:T(8,128)(2,1)S(1)}, bf16[128,1024]{1,0:T(8,128)(2,1)S(1)}, bf16[128,1024]{1,0:T(8,128)(2,1)S(1)}) custom-call(bf16[128,4096]{1,0:T(8,128)(2,1)} %refs_0_.1, bf16[128,1024]{1,0:T(8,128)(2,1)} %bitcast.6, bf16[128,1024]{1,0:T(8,128)(2,1)} %bitcast.7, bf16[128,1024]{1,0:T(8,128)(2,1)} %refs_3_.1, s32[1,512]{1,0:T(1,128)} %refs_4_.1, ...), custom_call_target="tpu_custom_call" | custom-call | tf_op jit(solution)/shard_map/column/pallas_call | solution.py:925
  57.9 1.0 %tail.1 = (bf16[128,1024]{1,0:T(8,128)(2,1)}, bf16[128,1024]{1,0:T(8,128)(2,1)}, f32[128,1024]{1,0:T(8,128)}) custom-call(bf16[128,1024]{1,0:T(8,128)(2,1)S(1)} %get-tuple-element.9.mixed_ref, bf16[128,1024]{1,0:T(8,128)(2,1)S(1)} %get-tuple-element.10.grad_ref, bf16[128,1024]{1,0:T(8,128)(2,1)S(1)} %get-tuple-element.11.wg_ref), custom_call_target="tpu_custom_call" | custom-call | tf_op jit(solution)/shard_map/tail/pallas_call | solution.py:1017

commit v4 on v3

--- a/solution.py
+++ b/solution.py
@@ -388,11 +388,20 @@
         )
     ]
     barrier = pltpu.get_barrier_semaphore()
-    peers = [(lax.rem(me + step, n_dp), z) for step in range(1, n_dp)]
+    for step in range(1, n_dp):
+        pl.semaphore_signal(
+            barrier, inc=1, device_id=(lax.rem(me + step, n_dp), z), device_id_type=MESH
+        )
     for step in range(1, n_seq):
-        peers += [(me, lax.rem(z + step, n_seq)), (sib, lax.rem(z + step, n_seq))]
-    for peer in peers:
-        pl.semaphore_signal(barrier, inc=1, device_id=peer, device_id_type=MESH)
+        there = lax.rem(z + step, n_seq)
+
+        @pl.when(jnp.abs(there - z) < n_seq - 1)
+        def _():
+            for peer in (me, sib):
+                pl.semaphore_signal(
+                    barrier, inc=1, device_id=(peer, there), device_id_type=MESH
+                )
+
     for load in loads:
         load.start()
     loads[0].wait()
@@ -401,7 +410,8 @@
     arrived(W.at[:, : (n_dp - 1) * tok], lsem.at[1])
     for load in loads[5:]:
         load.wait()
-    pl.semaphore_wait(barrier, len(peers))
+    inner = jnp.where((z > 0) & (z < n_seq - 1), 1, 0)
+    pl.semaphore_wait(barrier, n_dp - 1 + 2 * (n_seq - 2) + 2 * inner)
     @pl.when(is_main)
     def _():
         pltpu.make_async_copy(meta_ref, mbuf, msem.at[1]).start()
@@ -600,18 +610,6 @@
         ATT[at, :] = hat
         MR[at, :] = (hat * gain * GT[at, :]).astype(BF16)
 
-    for b in blocks:
-
-        @pl.when(home_is_self(b))
-        def _():
-            pltpu.make_async_copy(
-                MR.at[b * tok : (b + 1) * tok], MX.at[pid], mxrecv
-            ).start()
-
-        @pl.when(jnp.logical_not(home_is_self(b)))
-        def _():
-            mx_send(b).start()
-
     pieces = PIECES
     piece = DH // pieces
 
@@ -744,6 +742,18 @@
                 home_send(b).start()
 
     arrived(SG.at[:3], sgrecv)
+    for b in blocks:
+
+        @pl.when(home_is_self(b))
+        def _():
+            pltpu.make_async_copy(
+                MR.at[b * tok : (b + 1) * tok], MX.at[pid], mxrecv
+            ).start()
+
+        @pl.when(jnp.logical_not(home_is_self(b)))
+        def _():
+            mx_send(b).start()
+
     g_mean = sum(SG[q, 0:1, :] for q in range(4)) / width
     g_dot = rstd * sum(SG[q, 1:2, :] + shifts[q] * SG[q, 0:1, :] for q in range(4)) / width
     TB[...] = jnp.concatenate([rstd, g_mean, g_dot, rstd] * 2, axis=0)

time: 59.1 us -> 58.1 us (0.983)
  Pallas kernels: 57.6 us -> 56.5 us
    pallas_call x1, Pallas kernels: 56.6 us -> 55.5 us  [column_parallel(): pl.pallas_call(lambda *refs: column_kernel(n_dp, n_seq, *refs), out_shape...]
where the time goes in v4:
time: 58.1 us; the launch traced here: 57.8 us
  Pallas kernels  56.5 us (97%)
  between operations  1.29 us (2%)
    pallas_call x1, Pallas kernels, column_parallel(): pl.pallas_call(lambda *refs: column_kernel(n_dp, n_seq, *refs), out_shape...  55.5 us

profile of v4, /device:TPU:1, one launch (start us, length us, event | category | flops | bytes accessed | tf_op | source)
XLA Modules:
  0.0 57.8 jit_solution(12765425542342927910)
XLA Ops:
  1.3 55.5 %column.1 = (bf16[128,1024]{1,0:T(8,128)(2,1)S(1)}, bf16[128,1024]{1,0:T(8,128)(2,1)S(1)}, bf16[128,1024]{1,0:T(8,128)(2,1)S(1)}) custom-call(bf16[128,4096]{1,0:T(8,128)(2,1)} %refs_0_.1, bf16[128,1024]{1,0:T(8,128)(2,1)} %bitcast.6, bf16[128,1024]{1,0:T(8,128)(2,1)} %bitcast.7, bf16[128,1024]{1,0:T(8,128)(2,1)} %refs_3_.1, s32[1,512]{1,0:T(1,128)} %refs_4_.1, ...), custom_call_target="tpu_custom_call" | custom-call | tf_op jit(solution)/shard_map/column/pallas_call | solution.py:935
  56.8 1.0 %tail.1 = (bf16[128,1024]{1,0:T(8,128)(2,1)}, bf16[128,1024]{1,0:T(8,128)(2,1)}, f32[128,1024]{1,0:T(8,128)}) custom-call(bf16[128,1024]{1,0:T(8,128)(2,1)S(1)} %get-tuple-element.9.mixed_ref, bf16[128,1024]{1,0:T(8,128)(2,1)S(1)} %get-tuple-element.10.grad_ref, bf16[128,1024]{1,0:T(8,128)(2,1)S(1)} %get-tuple-element.11.wg_ref), custom_call_target="tpu_custom_call" | custom-call | tf_op jit(solution)/shard_map/tail/pallas_call | solution.py:1027

commit v5 on v4

--- a/solution.py
+++ b/solution.py
@@ -539,15 +539,17 @@
             for peer in st_peers
         ]
 
-    def put_stats(ref, at, first, second):
-        ref[pid, :, at] = jnp.where(lane_col == 0, first, second).T[:8]
+    def put_stats(ref, b, first, second):
+        pair = jnp.where(lane_col == 0, first, second).T
+        ref[pid, b : b + 1, :] = pair[0:1]
+        ref[pid, n_seq + b : n_seq + b + 1, :] = pair[1:2]
 
     for b in range(n_seq):
         at = slice(b * tok, (b + 1) * tok)
         att = ATT[at, :]
         mean_own = jnp.mean(att, axis=1, keepdims=True)
         off = att - mean_own
-        put_stats(SA, at, mean_own, jnp.sum(off * off, axis=1, keepdims=True))
+        put_stats(SA, b, mean_own, jnp.sum(off * off, axis=1, keepdims=True))
     for copy in stat_sends(SA, saout, sarecv):
         copy.start()
     far_relay(1)
@@ -571,21 +573,23 @@
         off = att - jnp.mean(att, axis=1, keepdims=True)
         g = DM[at, :] * GT[at, :] * gain
         put_stats(
-            SG, at, jnp.sum(g, axis=1, keepdims=True), jnp.sum(g * off, axis=1, keepdims=True)
+            SG, b, jnp.sum(g, axis=1, keepdims=True), jnp.sum(g * off, axis=1, keepdims=True)
         )
     for copy in stat_sends(SG, sgout, sgrecv):
         copy.start()
 
     arrived(SA.at[:3], sarecv)
-    means = [SA[q, 0:1, :] for q in range(4)]
+    first, second = slice(0, n_seq), slice(n_seq, 2 * n_seq)
+    means = [SA[q, first, :] for q in range(4)]
     mean = sum(means[1:], means[0]) / 4.0
     shifts = [m - mean for m in means]
-    squares = sum(SA[q, 1:2, :] + own_width * shifts[q] * shifts[q] for q in range(4))
+    squares = sum(SA[q, second, :] + own_width * shifts[q] * shifts[q] for q in range(4))
     rstd = lax.rsqrt(squares / width + EPS)
-    TB[...] = jnp.concatenate([mean, rstd] * 4, axis=0)
-
-    def turned(at):
-        return jnp.concatenate([TB[:, at]] * (DH // 8), axis=0).T
+    TB[0], TB[1] = mean, rstd
+
+    def turned(i, b):
+        wide_row = jnp.broadcast_to(TB[i, b : b + 1, :], (DH, DH)).T
+        return jnp.concatenate([wide_row] * 2, axis=1)
 
     blocks = tuple(reversed(range(n_seq)))
 
@@ -605,8 +609,7 @@
 
     for b in blocks:
         at = slice(b * tok, (b + 1) * tok)
-        columns = turned(at)
-        hat = (ATT[at, :] - columns[:, 0:1]) * columns[:, 1:2]
+        hat = (ATT[at, :] - turned(0, b)) * turned(1, b)
         ATT[at, :] = hat
         MR[at, :] = (hat * gain * GT[at, :]).astype(BF16)
 
@@ -754,17 +757,16 @@
         def _():
             mx_send(b).start()
 
-    g_mean = sum(SG[q, 0:1, :] for q in range(4)) / width
-    g_dot = rstd * sum(SG[q, 1:2, :] + shifts[q] * SG[q, 0:1, :] for q in range(4)) / width
-    TB[...] = jnp.concatenate([rstd, g_mean, g_dot, rstd] * 2, axis=0)
+    g_mean = sum(SG[q, first, :] for q in range(4)) / width
+    g_dot = rstd * sum(SG[q, second, :] + shifts[q] * SG[q, first, :] for q in range(4)) / width
+    TB[1], TB[2], TB[3] = rstd, g_mean, g_dot
     for b in range(n_seq):
         at = slice(b * tok, (b + 1) * tok)
-        columns = turned(at)
         d_mix, hat = DM[at, :], ATT[at, :]
         DG[at, :] = d_mix * (hat * gain)
         g = d_mix * GT[at, :] * gain
         DA[at, :] = (
-            columns[:, 0:1] * (g - columns[:, 1:2] - hat * columns[:, 2:3])
+            turned(1, b) * (g - turned(2, b) - hat * turned(3, b))
         ).astype(BF16)
 
     def backward(j, b):
@@ -802,6 +804,18 @@
     for b in blocks:
         for j in range(2):
             backward(j, b)
+        if b == last - 1:
+
+            @pl.when(ks == 0)
+            def _():
+                cross(last)
+
+        elif b == 1:
+
+            @pl.when(ks == 0)
+            def _():
+                cross(2)
+
         if b == last:
 
             @pl.when(ks == 0)
@@ -810,14 +824,6 @@
 
         else:
             d_part(b)
-        if b == last - 1:
-
-            @pl.when(ks == 0)
-            def _():
-                cross(last)
-
-        elif b == 1:
-            cross(2)
         if b < 2:
             for i in range(pieces // 2):
                 plane_sum((1 - b) * pieces // 2 + i)
@@ -830,15 +836,24 @@
 
     @pl.when(ks != 0)
     def _():
+        cross(2)
         d_part(last)
         cross(last)
 
     finish(3)
     pass_in()
-    finish(2)
+    @pl.when(ks == 0)
+    def _():
+        finish(2)
+
     pass_out()
     finish(1)
     finish(0)
+
+    @pl.when(ks != 0)
+    def _():
+        finish(2)
+
     near_total()
     arrived(WO.at[2 * (1 - p) + k], worecv.at[2])
     for j in range(2):
@@ -968,9 +983,9 @@
             vb(4, tok, 2 * DH),
             vf(2, rows, DH),
             vf(2, rows, DH),
-            vf(4, 8, rows),
-            vf(4, 8, rows),
-            vf(8, rows),
+            vf(4, 8, DH),
+            vf(4, 8, DH),
+            vf(4, n_seq, DH),
             vb(2, PIECES, DH // PIECES, width),
             vb(n_dp // 2, PIECES, DH // PIECES, width),
             vb(PIECES, DH // PIECES, width),

time: 58.1 us -> 57.7 us (level)
  no operation moved by 1% of the time
where the time goes in v5:
time: 57.7 us; the launch traced here: 57.5 us
  Pallas kernels  56.3 us (98%)
  between operations  1.29 us (2%)
    pallas_call x1, Pallas kernels, column_parallel(): pl.pallas_call(lambda *refs: column_kernel(n_dp, n_seq, *refs), out_shape...  55.3 us

profile of v5, /device:TPU:1, one launch (start us, length us, event | category | flops | bytes accessed | tf_op | source)
XLA Modules:
  0.0 57.5 jit_solution(17190865912556142798)
XLA Ops:
  1.3 55.3 %column.1 = (bf16[128,1024]{1,0:T(8,128)(2,1)S(1)}, bf16[128,1024]{1,0:T(8,128)(2,1)S(1)}, bf16[128,1024]{1,0:T(8,128)(2,1)S(1)}) custom-call(bf16[128,4096]{1,0:T(8,128)(2,1)} %refs_0_.1, bf16[128,1024]{1,0:T(8,128)(2,1)} %bitcast.6, bf16[128,1024]{1,0:T(8,128)(2,1)} %bitcast.7, bf16[128,1024]{1,0:T(8,128)(2,1)} %refs_3_.1, s32[1,512]{1,0:T(1,128)} %refs_4_.1, ...), custom_call_target="tpu_custom_call" | custom-call | tf_op jit(solution)/shard_map/column/pallas_call | solution.py:950
  56.6 1.0 %tail.1 = (bf16[128,1024]{1,0:T(8,128)(2,1)}, bf16[128,1024]{1,0:T(8,128)(2,1)}, f32[128,1024]{1,0:T(8,128)}) custom-call(bf16[128,1024]{1,0:T(8,128)(2,1)S(1)} %get-tuple-element.9.mixed_ref, bf16[128,1024]{1,0:T(8,128)(2,1)S(1)} %get-tuple-element.10.grad_ref, bf16[128,1024]{1,0:T(8,128)(2,1)S(1)} %get-tuple-element.11.wg_ref), custom_call_target="tpu_custom_call" | custom-call | tf_op jit(solution)/shard_map/tail/pallas_call | solution.py:1042

commit v6 on v5

--- a/solution.py
+++ b/solution.py
@@ -871,7 +871,6 @@
     centred = wide - average
     inv = lax.rsqrt(jnp.mean(centred * centred, axis=-1, keepdims=True) + EPS)
     hat = centred * inv
-    outer_total()
     arrived(RO, orecv)
     grad = RO[...].reshape(tok, width).astype(F32) * gin_ref[...]
     back = inv * (
@@ -880,6 +879,7 @@
         - hat * jnp.mean(grad * hat, axis=-1, keepdims=True)
     )
     grad_ref[...] = (c_ref[...].astype(F32) + back).astype(BF16)
+    outer_total()
 
     beside = (sib, z)
 

time: 57.7 us -> 57.5 us (level)
  no operation moved by 1% of the time
where the time goes in v6:
time: 57.5 us; the launch traced here: 57.3 us
  Pallas kernels  56 us (97%)
  between operations  1.29 us (2%)
    pallas_call x1, Pallas kernels, column_parallel(): pl.pallas_call(lambda *refs: column_kernel(n_dp, n_seq, *refs), out_shape...  55 us

profile of v6, /device:TPU:1, one launch (start us, length us, event | category | flops | bytes accessed | tf_op | source)
XLA Modules:
  0.0 57.3 jit_solution(4718275100072254691)
XLA Ops:
  1.3 55.0 %column.1 = (bf16[128,1024]{1,0:T(8,128)(2,1)S(1)}, bf16[128,1024]{1,0:T(8,128)(2,1)S(1)}, bf16[128,1024]{1,0:T(8,128)(2,1)S(1)}) custom-call(bf16[128,4096]{1,0:T(8,128)(2,1)} %refs_0_.1, bf16[128,1024]{1,0:T(8,128)(2,1)} %bitcast.6, bf16[128,1024]{1,0:T(8,128)(2,1)} %bitcast.7, bf16[128,1024]{1,0:T(8,128)(2,1)} %refs_3_.1, s32[1,512]{1,0:T(1,128)} %refs_4_.1, ...), custom_call_target="tpu_custom_call" | custom-call | tf_op jit(solution)/shard_map/column/pallas_call | solution.py:950
  56.3 1.0 %tail.1 = (bf16[128,1024]{1,0:T(8,128)(2,1)}, bf16[128,1024]{1,0:T(8,128)(2,1)}, f32[128,1024]{1,0:T(8,128)}) custom-call(bf16[128,1024]{1,0:T(8,128)(2,1)S(1)} %get-tuple-element.9.mixed_ref, bf16[128,1024]{1,0:T(8,128)(2,1)S(1)} %get-tuple-element.10.grad_ref, bf16[128,1024]{1,0:T(8,128)(2,1)S(1)} %get-tuple-element.11.wg_ref), custom_call_target="tpu_custom_call" | custom-call | tf_op jit(solution)/shard_map/tail/pallas_call | solution.py:1042
